TPU v7x, 128 devices: a whole 4x4x4 slice. The times are simulated.
128 devices in a mesh: expert: 16 (over z, x), tensor: 8 (over y, core).
Axes of the slice: x: 4, y: 4, z: 4, core: 2. Of those that a mesh axis runs over, the one named last changes fastest.
Arguments:
- tokens: bfloat16 [2048, 4096], P('expert'), may hold values from -6 to 6
- scores: float32 [2048, 8], P('expert'), may hold values from -6 to 6
- expert_ids: int32 [2048, 8], P('expert'), may hold values from 0 to 63, all different within a row; in each aligned block of 128 rows (0 to 127, 128 to 255, ...) at most 32 rows name the same one
- gate_weight: bfloat16 [64, 1536, 4096], P('expert', 'tensor'), may hold values from -0.09375 to 0.09375
- up_weight: bfloat16 [64, 1536, 4096], P('expert', 'tensor'), may hold values from -0.09375 to 0.09375
- down_weight: bfloat16 [64, 1536, 4096], P('expert', 'tensor'), may hold values from -0.15625 to 0.15625
Outputs:
- mixed: bfloat16 [2048, 4096], P('expert', 'tensor')
Inputs may be any that keep to these rules, and one draw needn't show every extreme that they name: `expert_ids`: each row names 8 different experts. Among the 128 rows of one owner (rows o * 128 to (o + 1) * 128 - 1) no expert is named more than 32 times.
All inputs are finite; a program needn't handle non-finite values.
Results may differ from a plain program's by a relative error of at most 0.018.
Values may be sent and summed in bfloat16 or wider, within the bound.
A program may use at most 128 MiB of HBM per device.

v0:
```python
import jax
import jax.numpy as jnp
from jax import lax
from jax.sharding import PartitionSpec as P

TOP = 8


def copy_for_each(x, axis):
    copies = jnp.broadcast_to(x, (lax.axis_size(axis), *x.shape))
    return lax.all_to_all(copies, axis, split_axis=0, concat_axis=0, tiled=True)


def in_order(parts, dim):
    dims = list(parts.shape[1:])
    dims[dim] *= parts.shape[0]
    return jnp.moveaxis(parts, 0, dim).reshape(dims)


def gathered_copies(x, axis, dim):
    parts = copy_for_each(x, axis)
    return in_order(parts, dim)


def gate_of(scores):
    lifted = jnp.exp(scores)
    return (lifted / jnp.sum(lifted, axis=-1, keepdims=True)).astype(jnp.bfloat16)


def slot_tables(expert_ids, gate_values, experts, blocks, capacity):
    rows_all = expert_ids.shape[0]
    block_rows = rows_all // blocks
    expert_count = experts.shape[0]
    matches = expert_ids[:, :, None] == experts[None, None, :]
    routed = jnp.any(matches, axis=1).astype(jnp.int32)
    chosen_gate = jnp.sum(
        jnp.where(matches, gate_values.astype(jnp.float32)[:, :, None], jnp.float32(0.0)), axis=1
    )
    folded = routed.reshape(blocks, block_rows, expert_count)
    rank_in_block = jnp.cumsum(folded, axis=1) - folded
    block_start = (jnp.arange(blocks, dtype=jnp.int32) * capacity)[:, None, None]
    slot_index = (block_start + rank_in_block).reshape(rows_all, expert_count)
    slot_index = jnp.where(routed == 1, slot_index, blocks * capacity)
    columns = jnp.broadcast_to(jnp.arange(expert_count, dtype=jnp.int32)[None, :], slot_index.shape)
    position = jnp.broadcast_to(jnp.arange(rows_all, dtype=jnp.int32)[:, None], slot_index.shape)
    slot_token = (
        jnp.full((expert_count, blocks * capacity), rows_all, jnp.int32)
        .at[columns, slot_index]
        .set(position, mode="drop")
    )
    slot_gate = (
        jnp.zeros((expert_count, blocks * capacity), jnp.float32)
        .at[columns, slot_index]
        .set(chosen_gate, mode="drop")
    )
    return (slot_token, slot_gate)


def local(tokens, scores, expert_ids, gate_weight, up_weight, down_weight):
    groups = lax.axis_size("expert")
    ranks = lax.axis_size("tensor")
    local_experts = gate_weight.shape[0]
    owner_rows = tokens.shape[0]
    width = tokens.shape[1]
    share = width // ranks
    capacity = 2 * owner_rows * TOP // (local_experts * groups)
    gate_values = gate_of(scores)
    all_ids = gathered_copies(expert_ids, "expert", 0)
    all_gates = gathered_copies(gate_values, "expert", 0)
    first_expert = lax.axis_index("expert") * local_experts
    held_experts = first_expert + jnp.arange(local_experts, dtype=jnp.int32)
    slot_token, slot_gate = slot_tables(all_ids, all_gates, held_experts, groups, capacity)
    send_order = (
        jnp.arange(local_experts, dtype=jnp.int32)[:, None]
        + local_experts * jnp.arange(groups, dtype=jnp.int32)[None, :]
    ).reshape(-1)
    send_token = slot_tables(expert_ids, gate_values, send_order, 1, capacity)[0]
    send_index = send_token.reshape(-1)
    column_start = lax.axis_index("tensor") * share
    narrow = lax.dynamic_slice_in_dim(tokens, column_start, share, 1)
    outgoing = jnp.take(narrow, send_index, axis=0, mode="fill", fill_value=0).reshape(
        local_experts, groups * capacity, share
    )
    arrived = lax.all_to_all(outgoing, "expert", split_axis=1, concat_axis=1, tiled=True)
    piece = lax.all_gather(arrived, "tensor", axis=2, tiled=True)
    gate_next = jnp.einsum("jcd,jfd->jcf", piece, gate_weight, preferred_element_type=jnp.float32)
    up_next = jnp.einsum("jcd,jfd->jcf", piece, up_weight, preferred_element_type=jnp.float32)
    hidden = (jax.nn.silu(gate_next) * up_next).astype(jnp.bfloat16)
    partial_value = jnp.einsum(
        "jcf,jfd->jcd", hidden, down_weight, preferred_element_type=jnp.float32
    ).astype(jnp.bfloat16)
    summed = lax.psum_scatter(partial_value, "tensor", scatter_dimension=2, tiled=True).astype(
        jnp.float32
    )
    gated = summed * slot_gate[:, :, None]
    returned = lax.all_to_all(
        gated.astype(jnp.bfloat16), "expert", split_axis=1, concat_axis=1, tiled=True
    ).astype(gated.dtype)
    mixed = (
        jnp.zeros((owner_rows, share), jnp.float32)
        .at[send_index]
        .add(returned.reshape(-1, share), mode="drop")
    )
    return mixed.astype(jnp.bfloat16)


def solution(mesh):
    in_specs = (
        P("expert", None),
        P("expert", None),
        P("expert", None),
        P("expert", "tensor", None),
        P("expert", "tensor", None),
        P("expert", "tensor", None),
    )
    out_specs = P("expert", "tensor")
    return jax.shard_map(local, mesh=mesh, in_specs=in_specs, out_specs=out_specs, check_vma=False)
```

profile of v0, /device:TPU:0, one launch (start us, length us, event | category | flops | bytes accessed | tf_op | source)
XLA Modules:
  0.0 369.7 jit_solution(3893563274801632213)
XLA Ops:
  6.5 0.0 copy-start
  6.5 0.0 all-gather.2.cloned.1.call-start
  6.6 0.1 add.116
  6.6 0.9 compare_reduce_fusion.1
  7.5 4.4 %copy.97 = s32[128,64,1]{2,1,0:T(8,128)} copy(s32[128,64,1]{0,1,2:T(8,128)S(1)} %convert_bitcast_fusion.2) | data formatting | bytes 65536 | tf_op jit(solution)/shard_map/convert_element_type | solution.py:35
  12.0 4.5 %fusion.14 = s32[128,64,1]{2,1,0:T(8,128)} fusion(s32[128,64,1]{2,1,0:T(8,128)} %copy.97), kind=kOutput, calls=%fused_computation.52 | output fusion | flops 1040384 | bytes 65536 | tf_op jit(solution)/shard_map/jit(cumsum)/reduce_window_sum | solution.py:40
  16.5 0.0 copy-start.6
  16.5 3.8 %copy.98 = s32[128,64,1]{0,1,2:T(8,128)S(1)} copy(s32[128,64,1]{2,1,0:T(8,128)} %fusion.14) | data formatting | bytes 65536 | tf_op jit(solution)/shard_map/jit(cumsum)/reduce_window_sum | solution.py:40
  20.2 0.0 copy-done.6
  20.3 0.1 multiply_reduce_fusion.1
  20.3 0.0 copy-done.7
  20.3 0.1 and_reduce_fusion.1
  20.4 0.1 copy.99
  20.5 0.1 reshape.257
  20.6 0.1 reshape.259
  20.7 30.4 %scatter_custom_fusion.1 = s32[2048]{0:T(1024)S(1)} fusion(s32[8192]{0:T(1024)S(1)} %reshape.257, s32[8192]{0:T(1024)S(1)} %reshape.259, s32[]{:T(128)} %constant.17.clone.1), kind=kCustom, calls=%fused_computation.41 | custom fusion | bytes 8196
  51.2 0.1 reshape.229
  51.2 0.1 copy.100
  51.3 0.1 reshape.223
  51.4 0.1 reshape.224
  51.5 0.2 copy.102
  51.7 0.0 copy-done
  51.8 7.5 %gather_fusion = bf16[2048,512]{1,0:T(8,128)(2,1)S(1)} fusion(bf16[128,512]{1,0:T(8,128)(2,1)S(1)} %constant_dynamic-slice_fusion, s32[2048]{0:T(1024)S(1)} %broadcast_clamp_fusion), kind=kCustom, calls=%fused_computation | custom fusion | bytes 4202496 | tf_op jit(solution)/shard_map/jit(_take)/gather | solution.py:81
  59.3 5.2 %copy_select_fusion = bf16[4,512,512]{2,0,1:T(4,128)(2,1)S(1)} fusion(bf16[4,512,512]{2,1,0:T(8,128)(2,1)S(1)} %bitcast.45, pred[4,512]{0,1:T(8,128)(4,1)S(1)} %copy.102), kind=kLoop, calls=%fused_computation.8 | loop fusion | flops 1048576 | bytes 4196352 | tf_op jit(solution)/shard_map/jit(_take)/select_n | solution.py:81
  64.5 36.2 %all_to_all.20 = bf16[4,512,512]{2,0,1:T(4,128)(2,1)S(1)} all-to-all(bf16[4,512,512]{2,0,1:T(4,128)(2,1)S(1)} %copy_select_fusion), channel_id=1, replica_groups=mesh['expert'=16,'tensor'=8] {'expert'}, dimensions={1} | all-to-all | bytes 4194304 | tf_op jit(solution)/shard_map/all_to_all | solution.py:84
  100.7 1.8 copy.104
  102.5 0.0 all-gather.2.cloned.1.call-update
  102.5 0.0 reduce-scatter.2.cloned.1.call-start
  102.5 82.7 %all-gather.2.cloned.1.call-done = bf16[4,512,4096]{2,1,0:T(8,128)(2,1)} async-done(((bf16[4,512,512]{2,1,0:T(8,128)(2,1)}), bf16[4,512,4096]{2,1,0:T(8,128)(2,1)}) %all-gather.2.cloned.1.call-update) | async-done | bytes 16777232 | tf_op jit(solution)/shard_map/all_gather | solution.py:85
  185.2 11.0 %fusion.16 = f32[4,512,192]{1,2,0:T(8,128)S(1)} fusion(bf16[4,512,4096]{2,1,0:T(8,128)(2,1)} %all-gather.2.cloned.1.call-done, bf16[4,192,4096]{2,1,0:T(8,128)(2,1)} %param.9), kind=kOutput, calls=%fused_computation.54 | convolution fusion | flops 3221225472 | bytes 24641536 | tf_op jit(solution)/shard_map/jcd,jfd->jcf/dot_general | solution.py:86
  196.2 21.6 %convolution_convert_fusion = bf16[4,512,4096]{2,1,0:T(8,128)(2,1)} fusion(bf16[4,192,4096]{2,1,0:T(8,128)(2,1)} %param.11, f32[4,512,192]{1,2,0:T(8,128)S(1)} %fusion.16, bf16[4,512,4096]{2,1,0:T(8,128)(2,1)} %all-gather.2.cloned.1.call-done, bf16[4,192,4096]{2,1,0:T(8,128)(2,1)} %param.10), kind=kOutput, calls=%fused_computation.4 | convolution fusion | flops 6453198848 | bytes 47710208 | tf_op jit(solution)/shard_map/jcf,jfd->jcd/dot_general | solution.py:89
  217.8 0.0 reduce-scatter.2.cloned.1.call-update
  217.9 0.7 copy-done.3
  218.6 0.6 broadcast_in_dim.87
  219.2 6.9 %all-to-all-start.2 = ((bf16[16,128,8]{1,2,0:T(8,128)(2,1)}), bf16[16,128,8]{1,2,0:T(8,128)(2,1)S(1)}, u32[]{:S(2)}, u32[]{:S(2)}) async-start(bf16[16,128,8]{1,2,0:T(8,128)(2,1)} %broadcast_in_dim.87), calls=%async_computation.3 | async-start | bytes 65536 | tf_op jit(solution)/shard_map/all_to_all | solution.py:11
  226.2 0.1 broadcast_bitcast_fusion
  226.2 7.5 %all-to-all-done.2 = bf16[16,128,8]{1,2,0:T(8,128)(2,1)S(1)} async-done(((bf16[16,128,8]{1,2,0:T(8,128)(2,1)}), bf16[16,128,8]{1,2,0:T(8,128)(2,1)S(1)}, u32[]{:S(2)}, u32[]{:S(2)}) %all-to-all-start.2) | async-done | bytes 32800 | tf_op jit(solution)/shard_map/all_to_all | solution.py:11
  233.7 0.0 copy-done.2
  233.7 0.6 broadcast_in_dim.85
  234.4 3.5 all-to-all-start.1
  237.9 7.6 %all-to-all-done.1 = s32[16,128,8]{1,2,0:T(8,128)S(1)} async-done(((s32[16,128,8]{1,2,0:T(8,128)}), s32[16,128,8]{1,2,0:T(8,128)S(1)}, u32[]{:S(2)}, u32[]{:S(2)}) %all-to-all-start.1) | async-done | bytes 65568 | tf_op jit(solution)/shard_map/all_to_all | solution.py:11
  245.5 0.2 compare_reduce_fusion
  245.7 0.5 copy.105
  246.2 23.3 %fusion.15 = s32[16,128,4]{2,0,1:T(8,128)S(1)} fusion(s32[16,128,4]{2,0,1:T(8,128)S(1)} %copy.105), kind=kOutput, calls=%fused_computation.53 | output fusion | flops 1040384 | bytes 65536 | tf_op jit(solution)/shard_map/jit(cumsum)/reduce_window_sum | solution.py:40
  269.5 0.4 copy.106
  270.0 0.0 copy-done.5
  270.1 0.1 multiply_reduce_fusion
  270.1 0.0 copy-done.4
  270.2 0.1 and_reduce_fusion
  270.3 0.4 copy.107
  270.7 0.6 reshape.263
  271.3 0.2 fusion.3
  271.5 0.4 copy.108
  271.8 0.6 reshape.265
  272.5 30.4 %scatter_custom_fusion.2 = f32[2048]{0:T(1024)S(1)} fusion(s32[8192]{0:T(1024)S(1)} %reshape.263, f32[8192]{0:T(1024)S(1)} %reshape.265, f32[]{:T(128)} %constant.16.clone.1), kind=kCustom, calls=%fused_computation.39 | custom fusion | bytes 8196
  302.9 7.4 %reduce-scatter.2.cloned.1.call-done = bf16[4,512,512]{2,1,0:T(8,128)(2,1)} async-done(((bf16[4,512,4096]{2,1,0:T(8,128)(2,1)}), bf16[4,512,512]{2,1,0:T(8,128)(2,1)}) %reduce-scatter.2.cloned.1.call-update) | async-done | bytes 2097168 | tf_op jit(solution)/shard_map/reduce_scatter | solution.py:92
  310.4 2.1 multiply_convert_fusion
  312.5 1.6 copy.109
  314.1 0.0 copy-start.1
  314.1 34.8 %all_to_all.21 = bf16[4,512,512]{2,0,1:T(4,128)(2,1)S(1)} all-to-all(bf16[4,512,512]{2,0,1:T(4,128)(2,1)S(1)} %copy.109), channel_id=1, replica_groups=mesh['expert'=16,'tensor'=8] {'expert'}, dimensions={1} | all-to-all | bytes 4194304 | tf_op jit(solution)/shard_map/all_to_all | solution.py:96
  348.9 0.4 copy.110
  349.3 12.9 %scatter_custom_fusion = f32[128,512]{1,0:T(8,128)S(1)} fusion(s32[2048]{0:T(1024)S(1)} %bitcast.52, bf16[2048,512]{1,0:T(8,128)(2,1)S(1)} %bitcast.46, f32[]{:T(128)} %constant.16.clone.1), kind=kCustom, calls=%fused_computation.5 | custom fusion | flops 2097152 | bytes 2359300 | tf_op jit(solution)/shard_map/scatter-add | solution.py:102
  362.2 0.7 convert_element_type.85
  362.9 0.0 copy-done.1
  (28 shorter events, 0.2 us)
Async XLA Ops:
  6.5 45.2 %copy-start = (bf16[128,4096]{1,0:T(8,128)(2,1)S(1)}, bf16[128,4096]{1,0:T(8,128)(2,1)}, u32[]{:S(2)}) copy-start(bf16[128,4096]{1,0:T(8,128)(2,1)} %param.6) | copy-start | bytes 3145732
  6.5 178.7 %all-gather.2.cloned.1.call-start = ((), (), s32[]{:S(2)}) async-start(), calls=%async_computation.5 | async-start | bytes 18874368 | tf_op jit(solution)/shard_map/all_gather | solution.py:85
  16.5 3.8 %copy-start.6 = (s32[2]{0:T(128)S(1)}, s32[2]{0:T(128)}, u32[]{:S(2)}) copy-start(s32[2]{0:T(128)} %constant.68) | copy-start | bytes 28
  16.5 3.9 %copy-start.7 = (s32[2]{0:T(128)S(1)}, s32[2]{0:T(128)}, u32[]{:S(2)}) copy-start(s32[2]{0:T(128)} %constant.71) | copy-start | bytes 28
  102.5 207.9 %reduce-scatter.2.cloned.1.call-start = ((), (), s32[]{:S(2)}) async-start(), calls=%async_computation.6 | async-start | bytes 18874368 | tf_op jit(solution)/shard_map/reduce_scatter | solution.py:92
  217.8 0.7 copy-start.3
  217.8 15.9 %copy-start.2 = (s32[128,8]{0,1:T(8,128)S(1)}, s32[128,8]{0,1:T(8,128)}, u32[]{:S(2)}) copy-start(s32[128,8]{0,1:T(8,128)} %param.8) | copy-start | bytes 12292
  218.5 51.5 %copy-start.5 = (s32[2]{0:T(128)S(1)}, s32[2]{0:T(128)}, u32[]{:S(2)}) copy-start(s32[2]{0:T(128)} %constant.74) | copy-start | bytes 28
  218.5 51.6 %copy-start.4 = (s32[2]{0:T(128)S(1)}, s32[2]{0:T(128)}, u32[]{:S(2)}) copy-start(s32[2]{0:T(128)} %constant.77) | copy-start | bytes 28
  219.2 14.6 %all-to-all-start.2 = ((bf16[16,128,8]{1,2,0:T(8,128)(2,1)}), bf16[16,128,8]{1,2,0:T(8,128)(2,1)S(1)}, u32[]{:S(2)}, u32[]{:S(2)}) async-start(bf16[16,128,8]{1,2,0:T(8,128)(2,1)} %broadcast_in_dim.87), calls=%async_computation.3 | async-start | bytes 65536 | tf_op jit(solution)/shard_map/all_to_all | solution.py:11
  234.4 11.1 %all-to-all-start.1 = ((s32[16,128,8]{1,2,0:T(8,128)}), s32[16,128,8]{1,2,0:T(8,128)S(1)}, u32[]{:S(2)}, u32[]{:S(2)}) async-start(s32[16,128,8]{1,2,0:T(8,128)} %broadcast_in_dim.85), calls=%async_computation.2 | async-start | bytes 131072 | tf_op jit(solution)/shard_map/all_to_all | solution.py:11
  314.1 48.8 %copy-start.1 = (bf16[128,4096]{1,0:T(8,128)(2,1)S(1)}, bf16[128,4096]{1,0:T(8,128)(2,1)}, u32[]{:S(2)}) copy-start(bf16[128,4096]{1,0:T(8,128)(2,1)} %param.6) | copy-start | bytes 3145732
Sparse Core Ops, SparseCore 0:
  102.6 82.5 all-gather.1
  218.0 92.3 reduce-scatter.1
where the time goes:
time: 371 us; the launch traced here: 370 us
  waiting for transfers between devices  105 us (28%)
  local copies, waits for them, and re-layouts  86.3 us (23%)
  blocking collectives  71 us (19%)
  other arithmetic  50.3 us (14%)
  matrix products  32.6 us (9%)
  between operations  13.7 us (4%)
  starting transfers between devices  10.5 us (3%)
    all_gather x1, waiting for transfers between devices, local(): piece = lax.all_gather(arrived, 'tensor', axis=2, tiled=True)  82.7 us
    unnamed x24, local copies, waits for them, and re-layouts  62.8 us
    all_to_all x1, blocking collectives, local(): lax.all_to_all(outgoing, 'expert', split_axis=1, concat_axis=1, tiled=True)  36.2 us
    all_to_all x1, blocking collectives, local(): lax.all_to_all(gated.astype(jnp.bfloat16), 'expert', split_axis=1, concat...  34.8 us
    another operation x2, other arithmetic, slot_tables(): rank_in_block = jnp.cumsum(folded, axis=1) - folded  27.8 us
    dot_general x1, matrix products, local(): jnp.einsum('jcf,jfd->jcd', hidden, down_weight, preferred_element_type=jn...  21.6 us
    all_to_all x2, waiting for transfers between devices, copy_for_each(): return lax.all_to_all(copies, axis, split_axis=0, concat_axis=0, tiled=True)  15.1 us
    scatter-add x1, other arithmetic, local(): mixed = jnp.zeros((owner_rows, share), jnp.float32).at[send_index].add(re...  12.9 us
  transfers between devices with their start and end apart: 4, of which 4 were waited for; matrix products, arithmetic and copies ran while one was open for 16% of the time, Pallas kernels for 0%

commit v1 on v0

v1 whole, which is shorter than its diff:
```python
import jax
import jax.numpy as jnp
from jax import lax
from jax.experimental import pallas as pl
from jax.experimental.pallas import tpu as pltpu
from jax.sharding import PartitionSpec as P

MESH = pl.DeviceIdType.MESH
f32 = jnp.float32
bf16 = jnp.bfloat16

RING = 4
OWN = 128
WIDTH = 4096
FFS = 192
HELD = 4
CAP = 32
QUART = 1024
INFO = 16
CHUNK = 512
BATCH = RING * OWN
ORDER = (2, 1, 3, 0)
NT = (((1,), (1,)), ((), ()))


def distance(kind, dz, dx):
    if kind == 0:
        return dx if dz == 0 else dz
    return dz if dx == 0 else dx


def transfer_ids():
    ids = {}
    for kind in range(2):
        for dz in range(RING):
            for dx in range(RING):
                if dz == 0 and dx == 0:
                    continue
                parts = ("h0", "h1") if distance(kind, dz, dx) == 2 else ("f",)
                for part in parts:
                    ids[kind, dz, dx, part] = len(ids)
                ids[kind, dz, dx, "d"] = len(ids)
    return ids


IDS = transfer_ids()


def kernel(
    tokens, info, wg_in, wu_in, wd_in, out,
    xa, xb, wg, wu, wd, rows, pmat, pgt, hid, part_buf, mine, theirs, dgot,
    y1got, y2got, tot, x1got, x2got, kept, leaving, zgot,
    lsem, ssem, rsem, d_s, d_r, y_s, y_r, x_s, x_r, z_s, z_r,
):
    me = lax.axis_index("expert")
    rank = lax.axis_index("tensor")
    z, x = me // RING, me % RING
    y, c = rank // 2, rank % 2
    other = 1 - c

    def device(dz, dx, dy, core):
        return (((z + dz) % RING) * RING + (x + dx) % RING, ((y + dy) % RING) * 2 + core)

    peers = [
        device(0, 1, 0, c), device(0, 3, 0, c), device(1, 0, 0, c), device(3, 0, 0, c),
        device(2, 0, 0, c), device(0, 0, 1, c), device(0, 0, 3, c), device(0, 0, 0, other),
    ]
    barrier = pltpu.get_barrier_semaphore()
    for peer in peers:
        pl.semaphore_signal(barrier, inc=1, device_id=peer, device_id_type=MESH)

    bufs = (xa, xb)
    loads = []

    def load(src, dst):
        copy = pltpu.make_async_copy(src, dst, lsem.at[len(loads)])
        loads.append(copy)
        copy.start()
        return copy

    own_loads = []
    for half in range(2):
        own_loads.append(load(tokens.at[:, pl.ds(half * 2048, QUART)], xa.at[half, me, pl.ds(0, OWN)]))
        own_loads.append(load(info, xa.at[half, me, pl.ds(OWN, INFO)]))
        own_loads.append(load(tokens.at[:, pl.ds(half * 2048 + QUART, QUART)], xb.at[half, me]))
    weight_loads = [load(wg_in, wg), load(wu_in, wu), load(wd_in, wd)]

    def view(kind, half, dz, dx, part):
        owner = ((z + dz) % RING) * RING + (x + dx) % RING
        buf = bufs[kind]
        if part == "h0":
            return buf.at[half, owner, pl.ds(0, 64)]
        if part == "h1":
            return buf.at[half, owner, pl.ds(64, buf.shape[2] - 64)]
        return buf.at[half, owner]

    started = {}

    def describe(kind, dz, dx, part, tz, tx):
        ident = IDS[kind, (dz - tz) % RING, (dx - tx) % RING, part]
        ref = view(kind, c, dz, dx, part)
        return pltpu.make_async_remote_copy(
            src_ref=ref, dst_ref=ref, send_sem=ssem.at[ident], recv_sem=rsem.at[ident],
            device_id=device(tz, tx, 0, c), device_id_type=MESH,
        )

    def send(kind, dz, dx, part, tz, tx):
        started[describe, (kind, dz, dx, part, tz, tx)] = True
        describe(kind, dz, dx, part, tz, tx).start()

    def describe_pair(kind, dz, dx, half=c):
        ident = IDS[kind, dz, dx, "d"]
        ref = view(kind, half, dz, dx, "f")
        return pltpu.make_async_remote_copy(
            src_ref=ref, dst_ref=ref, send_sem=ssem.at[ident], recv_sem=rsem.at[ident],
            device_id=device(0, 0, 0, other), device_id_type=MESH,
        )

    def pair(kind, dz, dx):
        started[describe_pair, (kind, dz, dx)] = True
        describe_pair(kind, dz, dx).start()

    def got_pair(kind, dz, dx):
        describe_pair(kind, dz, dx, other).wait_recv()

    def got(kind, dz, dx, part):
        ident = IDS[kind, dz, dx, part]
        ref = view(kind, c, dz, dx, part)
        pltpu.make_async_remote_copy(
            src_ref=ref, dst_ref=ref, send_sem=ssem.at[ident], recv_sem=rsem.at[ident],
            device_id=device(0, 0, 0, other), device_id_type=MESH,
        ).wait_recv()

    def along(kind, first, step):
        if (kind == 0) == first:
            return (0, step)
        return (step, 0)

    def arrive(kind, first, dz, dx):
        d = distance(kind, dz, dx)
        if d == 2:
            got(kind, dz, dx, "h0")
            got(kind, dz, dx, "h1")
        else:
            got(kind, dz, dx, "f")
            if d == 3:
                send(kind, dz, dx, "h0", *along(kind, first, 1))
            else:
                send(kind, dz, dx, "h1", *along(kind, first, 3))
        pair(kind, dz, dx)

    def spread(kind, first, dz, dx):
        for step in (1, 3):
            send(kind, dz, dx, "f", *along(kind, first, step))

    pl.semaphore_wait(barrier, len(peers))
    for copy in own_loads:
        copy.wait()
    spread(0, True, 0, 0)
    spread(1, True, 0, 0)
    spread(1, False, 0, 0)
    spread(0, False, 0, 0)
    for copy in weight_loads:
        copy.wait()

    arrive(0, True, 0, 3)
    arrive(0, True, 0, 1)
    arrive(1, True, 3, 0)
    arrive(1, True, 1, 0)
    arrive(1, False, 0, 3)
    arrive(1, False, 0, 1)
    spread(1, False, 1, 0)
    spread(1, False, 3, 0)
    spread(0, False, 0, 3)
    spread(0, False, 0, 1)
    arrive(0, True, 0, 2)
    spread(0, False, 0, 2)
    arrive(1, False, 0, 2)
    arrive(0, False, 1, 0)
    arrive(0, False, 3, 0)
    arrive(1, True, 2, 0)
    spread(1, False, 2, 0)

    def arrive_rest(dz):
        for dx in (3, 1):
            arrive(0, False, dz, dx)
            arrive(1, False, dz, dx)
        if dz == 2:
            arrive(0, False, 2, 0)
        arrive(0, False, dz, 2)
        arrive(1, False, dz, 2)

    def batch_z(b):
        return (b * (b + 1) // 2) % RING

    def slots(zz):
        earlier = lax.broadcasted_iota(jnp.int32, (OWN, OWN), 0)
        later = lax.broadcasted_iota(jnp.int32, (OWN, OWN), 1)
        triangle = jnp.where(earlier < later, 1.0, 0.0).astype(bf16)
        routed, gates = [], []
        for o in range(RING):
            facts = xa[0, zz * RING + o, pl.ds(OWN, INFO), pl.ds(0, OWN)].astype(f32)
            named, values = facts[0:8], facts[8:16]
            for j in range(HELD):
                match = named == (me * HELD + j).astype(f32)
                routed.append(jnp.max(jnp.where(match, 1.0, 0.0), axis=0, keepdims=True))
                gates.append(jnp.sum(jnp.where(match, values, 0.0), axis=0, keepdims=True))
        chosen = jnp.concatenate(routed, axis=0)
        place = jnp.dot(chosen.astype(bf16), triangle, preferred_element_type=f32)
        slot = lax.broadcasted_iota(jnp.int32, (CAP, OWN), 0).astype(f32)
        for o in range(RING):
            gated = []
            for j in range(HELD):
                i = o * HELD + j
                hit = jnp.where(slot == place[i : i + 1], 1.0, 0.0) * routed[i]
                pmat[o, pl.ds(j * CAP, CAP)] = hit.astype(bf16)
                gated.append(hit * gates[i])
            pgt[o] = jnp.concatenate(gated, axis=0).T.astype(bf16)

    def gather(zz):
        def one(o, carry):
            pick = pmat[o]
            for half in range(2):
                for kind in range(2):
                    block = bufs[kind][half, zz * RING + o, pl.ds(0, OWN)]
                    taken = jnp.dot(pick, block, preferred_element_type=f32).astype(bf16)
                    for e in range(HELD):
                        rows[e, pl.ds(o * CAP, CAP), pl.ds(half * 2048 + kind * QUART, QUART)] = taken[
                            e * CAP : (e + 1) * CAP
                        ]
            return carry

        lax.fori_loop(0, RING, one, 0)

    def experts():
        def one(e, carry):
            held = rows[e]
            gate = lax.dot_general(held, wg[e], NT, preferred_element_type=f32)
            up = lax.dot_general(held, wu[e], NT, preferred_element_type=f32)
            hid[e] = (gate * (1.0 / (1.0 + jnp.exp(-gate))) * up).astype(bf16)
            return carry

        lax.fori_loop(0, HELD, one, 0)

    def down(s, i, block, dst):
        column = pl.multiple_of(block * CHUNK, CHUNK)
        for e in range(HELD):
            value = jnp.dot(hid[e], wd[e, :, pl.ds(column, CHUNK)], preferred_element_type=f32).astype(bf16)
            for o in range(RING):
                part_buf[o, pl.ds(e * CAP, CAP)] = value[o * CAP : (o + 1) * CAP]
        for o in range(RING):
            dst[s, i, pl.ds(o * OWN, OWN)] = jnp.dot(
                pgt[o], part_buf[o], preferred_element_type=f32
            ).astype(bf16)

    def d_copy(s, i):
        return pltpu.make_async_remote_copy(
            src_ref=theirs.at[s, i], dst_ref=dgot.at[s, i], send_sem=d_s.at[s, i], recv_sem=d_r.at[s, i],
            device_id=device(0, 0, 0, other), device_id_type=MESH,
        )

    def y_copies(s, stage):
        if stage == 0:
            pieces = ((mine.at[s, 0, pl.ds(0, 256)], y1got.at[s, 0]), (mine.at[s, 0, pl.ds(256, 256)], y1got.at[s, 1]))
        else:
            pieces = ((mine.at[s, 1], y2got.at[s, 0]), (mine.at[s, 2], y2got.at[s, 1]))
        return [
            pltpu.make_async_remote_copy(
                src_ref=src, dst_ref=dst, send_sem=y_s.at[s, stage * 2 + n], recv_sem=y_r.at[s, stage * 2 + n],
                device_id=device(0, 0, (1, 3)[n], c), device_id_type=MESH,
            )
            for n, (src, dst) in enumerate(pieces)
        ]

    def owner_rows(dx, start, size):
        return pl.ds(pl.multiple_of(((x + dx) % RING) * OWN + start, 64), size)

    def x_copies(s, stage):
        if stage == 0:
            pieces = (
                (tot.at[s, owner_rows(2, 0, 64)], x1got.at[s, 0]),
                (tot.at[s, owner_rows(2, 64, 64)], x1got.at[s, 1]),
            )
        else:
            pieces = ((tot.at[s, owner_rows(1, 0, OWN)], x2got.at[s, 0]), (tot.at[s, owner_rows(3, 0, OWN)], x2got.at[s, 1]))
        return [
            pltpu.make_async_remote_copy(
                src_ref=src, dst_ref=dst, send_sem=x_s.at[s, stage * 2 + n], recv_sem=x_r.at[s, stage * 2 + n],
                device_id=device(0, (1, 3)[n], 0, c), device_id_type=MESH,
            )
            for n, (src, dst) in enumerate(pieces)
        ]

    def z_copy(i):
        b = i + 1
        return pltpu.make_async_remote_copy(
            src_ref=leaving.at[i], dst_ref=zgot.at[i], send_sem=z_s.at[i], recv_sem=z_r.at[i],
            device_id=device(batch_z(b), 0, 0, c), device_id_type=MESH,
        )

    def backs(s):
        for i, r in enumerate(ORDER):
            base = ((y + r) % RING) * 2
            down(s, i, base + other, theirs)
            d_copy(s, i).start()
            down(s, i, base + c, mine)
            d_copy(s, i).wait()
            mine[s, i] = (mine[s, i].astype(f32) + dgot[s, i].astype(f32)).astype(bf16)
            if i == 0:
                for copy in y_copies(s, 0):
                    copy.start()

    def y_second(s):
        for copy in y_copies(s, 0):
            copy.wait()
        lo, hi = pl.ds(0, 256), pl.ds(256, 256)
        mine[s, 1, lo] = (mine[s, 1, lo].astype(f32) + y1got[s, 0].astype(f32)).astype(bf16)
        mine[s, 2, hi] = (mine[s, 2, hi].astype(f32) + y1got[s, 1].astype(f32)).astype(bf16)
        for copy in y_copies(s, 1):
            copy.start()

    def y_third(s):
        for copy in y_copies(s, 1):
            copy.wait()
        tot[s] = (mine[s, 3].astype(f32) + y2got[s, 0].astype(f32) + y2got[s, 1].astype(f32)).astype(bf16)
        for copy in x_copies(s, 0):
            copy.start()

    def x_second(s):
        for copy in x_copies(s, 0):
            copy.wait()
        lo, hi = owner_rows(1, 0, 64), owner_rows(3, 64, 64)
        tot[s, lo] = (tot[s, lo].astype(f32) + x1got[s, 0].astype(f32)).astype(bf16)
        tot[s, hi] = (tot[s, hi].astype(f32) + x1got[s, 1].astype(f32)).astype(bf16)
        for copy in x_copies(s, 1):
            copy.start()

    def x_third(b, s):
        for copy in x_copies(s, 1):
            copy.wait()
        value = tot[s, owner_rows(0, 0, OWN)].astype(f32) + x2got[s, 0].astype(f32) + x2got[s, 1].astype(f32)

        @pl.when(b == 0)
        def _():
            kept[...] = value

        @pl.when(b > 0)
        def _():
            leaving[b - 1] = value.astype(bf16)
            z_copy(b - 1).start()

    def batch(b, carry):
        s = b % 2
        before = (b + 1) % 2
        dz = batch_z(b)
        zz = (z + dz) % RING
        for value in range(1, RING):
            step = batch_z(value)

            @pl.when(b == value)
            def _():
                if value == 1:
                    arrive_rest(1)
                    arrive_rest(3)
                if value == 3:
                    arrive_rest(2)
                for dx in range(RING):
                    got_pair(0, step, dx)
                    got_pair(1, step, dx)

        @pl.when(b == 0)
        def _():
            for dx in range(1, RING):
                got_pair(0, 0, dx)
                got_pair(1, 0, dx)

        slots(zz)
        gather(zz)

        @pl.when(b > 0)
        def _():
            y_second(before)

        experts()

        @pl.when(b > 1)
        def _():
            x_third(b - 2, s)

        backs(s)

        @pl.when(b > 0)
        def _():
            y_third(before)
            x_second(before)

        return carry

    lax.fori_loop(0, RING, batch, 0)
    y_second(1)
    x_third(2, 0)
    y_third(1)
    x_second(1)
    x_third(3, 1)
    total = kept[...]
    for i in range(3):
        z_copy(i).wait()
        total = total + zgot[i].astype(f32)
    out[...] = total.astype(bf16)
    for describe_one, args in started:
        describe_one(*args).wait_send()


def gate_of(scores):
    lifted = jnp.exp(scores)
    return (lifted / jnp.sum(lifted, axis=-1, keepdims=True)).astype(bf16)


def local(tokens, scores, expert_ids, gate_weight, up_weight, down_weight):
    info = jnp.concatenate([expert_ids.astype(bf16).T, gate_of(scores).T], axis=0)
    info = jnp.pad(info, ((0, 0), (0, QUART - OWN)))
    dma = pltpu.SemaphoreType.DMA
    count = len(IDS)
    return pl.pallas_call(
        kernel,
        out_shape=jax.ShapeDtypeStruct((OWN, CHUNK), bf16),
        in_specs=[pl.BlockSpec(memory_space=pl.ANY)] * 5,
        out_specs=pl.BlockSpec(memory_space=pltpu.VMEM),
        scratch_shapes=[
            pltpu.VMEM((2, 16, OWN + INFO, QUART), bf16),
            pltpu.VMEM((2, 16, OWN, QUART), bf16),
            pltpu.VMEM((HELD, FFS, WIDTH), bf16),
            pltpu.VMEM((HELD, FFS, WIDTH), bf16),
            pltpu.VMEM((HELD, FFS, WIDTH), bf16),
            pltpu.VMEM((HELD, OWN, WIDTH), bf16),
            pltpu.VMEM((RING, OWN, OWN), bf16),
            pltpu.VMEM((RING, OWN, OWN), bf16),
            pltpu.VMEM((HELD, OWN, FFS), bf16),
            pltpu.VMEM((RING, OWN, CHUNK), bf16),
            pltpu.VMEM((2, 4, BATCH, CHUNK), bf16),
            pltpu.VMEM((2, 4, BATCH, CHUNK), bf16),
            pltpu.VMEM((2, 4, BATCH, CHUNK), bf16),
            pltpu.VMEM((2, 2, BATCH // 2, CHUNK), bf16),
            pltpu.VMEM((2, 2, BATCH, CHUNK), bf16),
            pltpu.VMEM((2, BATCH, CHUNK), bf16),
            pltpu.VMEM((2, 2, OWN // 2, CHUNK), bf16),
            pltpu.VMEM((2, 2, OWN, CHUNK), bf16),
            pltpu.VMEM((OWN, CHUNK), f32),
            pltpu.VMEM((3, OWN, CHUNK), bf16),
            pltpu.VMEM((3, OWN, CHUNK), bf16),
            dma((9,)), dma((count,)), dma((count,)),
            dma((2, 4)), dma((2, 4)), dma((2, 4)), dma((2, 4)), dma((2, 4)), dma((2, 4)),
            dma((3,)), dma((3,)),
        ],
        compiler_params=pltpu.CompilerParams(
            collective_id=0, has_side_effects=True, vmem_limit_bytes=67043328
        ),
    )(tokens, info, gate_weight, up_weight, down_weight)


def solution(mesh):
    in_specs = (
        P("expert", None),
        P("expert", None),
        P("expert", None),
        P("expert", "tensor", None),
        P("expert", "tensor", None),
        P("expert", "tensor", None),
    )
    out_specs = P("expert", "tensor")
    return jax.shard_map(local, mesh=mesh, in_specs=in_specs, out_specs=out_specs, check_vma=False)
```

time: 371 us -> 161 us (0.43)
  Pallas kernels: 0 us -> 157 us
  waiting for transfers between devices: 105 us -> 0 us
  local copies, waits for them, and re-layouts: 86.3 us -> 1.57 us
  blocking collectives: 71 us -> 0 us
  other arithmetic: 50.3 us -> 2.71 us
  matrix products: 32.6 us -> 0 us
  between operations: 13.7 us -> 0.01 us
  starting transfers between devices: 10.5 us -> 0 us
    pallas_call x0 -> x1, Pallas kernels: none -> 157 us  [local(): pl.pallas_call(kernel, out_shape=jax.ShapeDtypeStruct((OWN, CHUNK), bf16)...]
    all_gather x1 -> x0, waiting for transfers between devices: 82.7 us -> none  [local(): piece = lax.all_gather(arrived, 'tensor', axis=2, tiled=True)]
    all_to_all x2 -> x0, blocking collectives: 71 us -> none  [the longest x1 36.2 us: local(): lax.all_to_all(outgoing, 'expert', split_axis=1, concat_axis=1, tiled=True)]
    unnamed x24 -> x1, local copies, waits for them, and re-layouts: 62.8 us -> 1.57 us
    dot_general x2 -> x0, matrix products: 32.6 us -> none  [the longest x1 21.6 us: local(): jnp.einsum('jcf,jfd->jcd', hidden, down_weight, preferred_element_type=jn...]
    another operation x2 -> x0, other arithmetic: 27.8 us -> none  [slot_tables(): rank_in_block = jnp.cumsum(folded, axis=1) - folded]
    all_to_all x2 -> x0, waiting for transfers between devices: 15.1 us -> none  [copy_for_each(): return lax.all_to_all(copies, axis, split_axis=0, concat_axis=0, tiled=True)]
    scatter-add x1 -> x0, other arithmetic: 12.9 us -> none  [local(): mixed = jnp.zeros((owner_rows, share), jnp.float32).at[send_index].add(re...]
  transfers between devices with their start and end apart: 4 -> 0, of which waited for: 4 -> 0; matrix products, arithmetic and copies ran while one was open for 16% -> 0% of each run, Pallas kernels for 0% -> 0%
where the time goes in v1:
time: 161 us
  Pallas kernels  157 us (98%)
  other arithmetic  2.71 us (2%)
    pallas_call x1, Pallas kernels, local(): pl.pallas_call(kernel, out_shape=jax.ShapeDtypeStruct((OWN, CHUNK), bf16)...  157 us

profile of v1, /device:TPU:0, one launch (start us, length us, event | category | flops | bytes accessed | tf_op | source)
XLA Modules:
  0.0 161.0 jit_solution(16350785256467216868)
XLA Ops:
  0.0 0.7 exponential_reduce_fusion
  0.7 0.7 fusion.3
  1.4 0.7 convert_bitcast_fusion
  2.1 0.6 fusion.2.info
  2.7 156.7 %shard_map.64 = bf16[128,512]{1,0:T(8,128)(2,1)} custom-call(bf16[128,4096]{1,0:T(8,128)(2,1)} %tokens.1, bf16[16,1024]{1,0:T(8,128)(2,1)} %fusion.2.info, bf16[4,192,4096]{2,1,0:T(8,128)(2,1)} %wg_in.1, bf16[4,192,4096]{2,1,0:T(8,128)(2,1)} %wu_in.1, bf16[4,192,4096]{2,1,0:T(8,128)(2,1)} %wd_in.1), custom_call_target="tpu_custom_call" | custom-call | tf_op jit(solution)/shard_map/pallas_call | solution.py:424
  159.4 1.6 copy.8

commit v2 on v0

v2 whole, which is shorter than its diff:
```python
import jax
import jax.numpy as jnp
from jax import lax
from jax.experimental import pallas as pl
from jax.experimental.pallas import tpu as pltpu
from jax.sharding import PartitionSpec as P

MESH = pl.DeviceIdType.MESH
f32 = jnp.float32
bf16 = jnp.bfloat16

RING = 4
OWN = 128
WIDTH = 4096
FFS = 192
HELD = 4
QUART = 1024
INFO = 16
CHUNK = 512
HID = HELD * FFS
TILE = 256
LANES = 256
BATCH = RING * OWN
ORDER = (2, 1, 3, 0)
NT = (((1,), (1,)), ((), ()))


def distance(kind, dz, dx):
    if kind == 0:
        return dx if dz == 0 else dz
    return dz if dx == 0 else dx


def transfer_ids():
    ids = {}
    for kind in range(2):
        for dz in range(RING):
            for dx in range(RING):
                if dz == 0 and dx == 0:
                    continue
                parts = ("h0", "h1") if distance(kind, dz, dx) == 2 else ("f",)
                for part in parts:
                    ids[kind, dz, dx, part] = len(ids)
                ids[kind, dz, dx, "d"] = len(ids)
    return ids


IDS = transfer_ids()


def scoped(name):
    def wrap(body):
        def inner(*args):
            with jax.named_scope(name):
                return body(*args)

        return inner

    return wrap


def kernel(
    tokens, info, wg_in, wu_in, wd_in, out,
    xa, xb, wg, wu, wd, hid, gx, mine, theirs, dgot,
    y1a, y1b, y2a, y2b, tota, totb, xsa, xsb, xg1, xg2, wrow, ys, kept, leave_y, leave_x, zy, zx,
    lsem, ssem, rsem, d_s, d_r, q_s, q_r,
):
    me = lax.axis_index("expert")
    rank = lax.axis_index("tensor")
    z, x = me // RING, me % RING
    y, c = rank // 2, rank % 2
    other = 1 - c

    def device(dz, dx, dy, core):
        return (((z + dz) % RING) * RING + (x + dx) % RING, ((y + dy) % RING) * 2 + core)

    peers = [device(0, 0, 0, other)]
    for step in (1, 3, 2):
        peers += [device(0, step, 0, c), device(step, 0, 0, c), device(0, 0, step, c)]
    barrier = pltpu.get_barrier_semaphore()
    for peer in peers:
        pl.semaphore_signal(barrier, inc=1, device_id=peer, device_id_type=MESH)

    bufs = (xa, xb)
    loads = []

    def load(src, dst):
        copy = pltpu.make_async_copy(src, dst, lsem.at[len(loads)])
        loads.append(copy)
        copy.start()
        return copy

    own_loads = []
    for half in range(2):
        own_loads.append(load(tokens.at[:, pl.ds(half * 2048, QUART)], xa.at[half, me, pl.ds(0, OWN)]))
        own_loads.append(load(info, xa.at[half, me, pl.ds(OWN, INFO)]))
        own_loads.append(load(tokens.at[:, pl.ds(half * 2048 + QUART, QUART)], xb.at[half, me]))
    weight_loads = [load(wg_in, wg), load(wu_in, wu), load(wd_in, wd)]

    def view(kind, half, dz, dx, part):
        owner = ((z + dz) % RING) * RING + (x + dx) % RING
        buf = bufs[kind]
        if part == "h0":
            return buf.at[half, owner, pl.ds(0, 64)]
        if part == "h1":
            return buf.at[half, owner, pl.ds(64, buf.shape[2] - 64)]
        return buf.at[half, owner]

    started = {}

    def describe(kind, dz, dx, part, tz, tx):
        ident = IDS[kind, (dz - tz) % RING, (dx - tx) % RING, part]
        ref = view(kind, c, dz, dx, part)
        return pltpu.make_async_remote_copy(
            src_ref=ref, dst_ref=ref, send_sem=ssem.at[ident], recv_sem=rsem.at[ident],
            device_id=device(tz, tx, 0, c), device_id_type=MESH,
        )

    def send(kind, dz, dx, part, tz, tx):
        started[describe, (kind, dz, dx, part, tz, tx)] = True
        describe(kind, dz, dx, part, tz, tx).start()

    def describe_pair(kind, dz, dx, half=c):
        ident = IDS[kind, dz, dx, "d"]
        ref = view(kind, half, dz, dx, "f")
        return pltpu.make_async_remote_copy(
            src_ref=ref, dst_ref=ref, send_sem=ssem.at[ident], recv_sem=rsem.at[ident],
            device_id=device(0, 0, 0, other), device_id_type=MESH,
        )

    def pair(kind, dz, dx):
        started[describe_pair, (kind, dz, dx)] = True
        describe_pair(kind, dz, dx).start()

    def got_pair(kind, dz, dx):
        describe_pair(kind, dz, dx, other).wait_recv()

    def got(kind, dz, dx, part):
        ident = IDS[kind, dz, dx, part]
        ref = view(kind, c, dz, dx, part)
        pltpu.make_async_remote_copy(
            src_ref=ref, dst_ref=ref, send_sem=ssem.at[ident], recv_sem=rsem.at[ident],
            device_id=device(0, 0, 0, other), device_id_type=MESH,
        ).wait_recv()

    def along(kind, first, step):
        if (kind == 0) == first:
            return (0, step)
        return (step, 0)

    def arrive(kind, first, dz, dx):
        d = distance(kind, dz, dx)
        if d == 2:
            got(kind, dz, dx, "h0")
            got(kind, dz, dx, "h1")
        else:
            got(kind, dz, dx, "f")
            if d == 3:
                send(kind, dz, dx, "h0", *along(kind, first, 1))
            else:
                send(kind, dz, dx, "h1", *along(kind, first, 3))
        pair(kind, dz, dx)

    def spread(kind, first, dz, dx):
        for step in (1, 3):
            send(kind, dz, dx, "f", *along(kind, first, step))

    def pairs(dz):
        for dx in range(RING):
            if dz or dx:
                got_pair(0, dz, dx)
                got_pair(1, dz, dx)

    queue_ids = {}

    def queued(key, src, dst, to):
        ident = queue_ids.setdefault(key, len(queue_ids))
        return pltpu.make_async_remote_copy(
            src_ref=src, dst_ref=dst, send_sem=q_s.at[ident], recv_sem=q_r.at[ident],
            device_id=to, device_id_type=MESH,
        )

    def begin(copies):
        for copy in copies:
            copy.start()

    def finish(copies):
        for copy in copies:
            copy.wait()

    def batch_z(b):
        return (b * (b + 1) // 2) % RING

    def wide(b):
        return CHUNK if b == 0 else LANES

    def y1(b):
        return y1a if b == 0 else y1b.at[b - 1]

    def y2(b):
        return y2a if b == 0 else y2b.at[b - 1]

    def tot(b):
        return tota if b == 0 else totb.at[b - 1]

    def xs(b):
        return xsa if b == 0 else xsb.at[b - 1]

    def owner_rows(dx, start, size):
        return pl.ds(pl.multiple_of(((x + dx) % RING) * OWN + start, 64), size)

    def y_copies(b, stage):
        lanes = pl.ds(0, wide(b))
        if stage == 0:
            pieces = [(mine.at[b % 3, 0, pl.ds(n * 256, 256), lanes], y1(b).at[n]) for n in range(2)]
        else:
            pieces = [(mine.at[b % 3, 1 + n, :, lanes], y2(b).at[n]) for n in range(2)]
        return [
            queued(("y", b, stage, n), src, dst, device(0, 0, (1, 3)[n], c)) for n, (src, dst) in enumerate(pieces)
        ]

    def y_last(b):
        return [
            queued(("ylast", b, d), tot(b).at[owner_rows(d, 0, OWN)], xs(b).at[d - 1], device(0, d, 0, c))
            for d in (2, 1, 3)
        ]

    @scoped("y_first")
    def y_first(b):
        begin(y_copies(b, 0))

    @scoped("y_second")
    def y_second(b):
        finish(y_copies(b, 0))
        lanes = pl.ds(0, wide(b))
        for n in range(2):
            rows = pl.ds(n * 256, 256)
            mine[b % 3, 1 + n, rows, lanes] = (
                mine[b % 3, 1 + n, rows, lanes].astype(f32) + y1(b)[n].astype(f32)
            ).astype(bf16)
        begin(y_copies(b, 1))

    @scoped("y_third")
    def y_third(b):
        finish(y_copies(b, 1))
        tot(b)[...] = (
            mine[b % 3, 3, :, pl.ds(0, wide(b))].astype(f32) + y2(b)[0].astype(f32) + y2(b)[1].astype(f32)
        ).astype(bf16)
        begin(y_last(b))

    def z_copy(b, part):
        src, dst = ((leave_y, zy), (leave_x, zx))[part]
        return queued(("z", b, part), src.at[b - 1], dst.at[b - 1], device(batch_z(b), 0, 0, c))

    @scoped("y_final")
    def y_final(b):
        finish(y_last(b))
        value = tot(b)[owner_rows(0, 0, OWN)].astype(f32)
        for n in range(3):
            value = value + xs(b)[n].astype(f32)
        if b == 0:
            kept[...] = value
        else:
            leave_y[b - 1] = value.astype(bf16)
            z_copy(b, 0).start()

    upper = pl.ds(LANES, LANES)

    def x_copies(b, stage):
        if stage == 0:
            pieces = [(mine.at[b % 3, :, owner_rows(2, 64 * n, 64), upper], xg1.at[b - 1, n]) for n in range(2)]
        else:
            pieces = [(mine.at[b % 3, :, owner_rows((1, 3)[n], 0, OWN), upper], xg2.at[b - 1, n]) for n in range(2)]
        return [
            queued(("x", b, stage, n), src, dst, device(0, (1, 3)[n], 0, c)) for n, (src, dst) in enumerate(pieces)
        ]

    def x_last(b):
        return [
            queued(("xlast", b, i), wrow.at[b - 1, i], ys.at[b - 1, i], device(0, 0, ORDER[i], c)) for i in range(3)
        ]

    @scoped("x_first")
    def x_first(b):
        begin(x_copies(b, 0))

    @scoped("x_second")
    def x_second(b):
        finish(x_copies(b, 0))
        for n in range(2):
            rows = owner_rows((1, 3)[n], 64 * n, 64)
            for i in range(4):
                mine[b % 3, i, rows, upper] = (
                    mine[b % 3, i, rows, upper].astype(f32) + xg1[b - 1, n, i].astype(f32)
                ).astype(bf16)
        begin(x_copies(b, 1))

    @scoped("x_third")
    def x_third(b):
        finish(x_copies(b, 1))
        rows = owner_rows(0, 0, OWN)
        for i in range(4):
            wrow[b - 1, i] = (
                mine[b % 3, i, rows, upper].astype(f32) + xg2[b - 1, 0, i].astype(f32) + xg2[b - 1, 1, i].astype(f32)
            ).astype(bf16)
        begin(x_last(b))

    @scoped("x_final")
    def x_final(b):
        finish(x_last(b))
        value = wrow[b - 1, 3].astype(f32)
        for i in range(3):
            value = value + ys[b - 1, i].astype(f32)
        leave_x[b - 1] = value.astype(bf16)
        z_copy(b, 1).start()

    @scoped("gates")
    def gates(zz):
        member = lax.broadcasted_iota(jnp.int32, (8, HID), 0)
        unit = lax.broadcasted_iota(jnp.int32, (8, HID), 1)
        expand = jnp.where((unit >= member * FFS) & (unit < member * FFS + FFS), 1.0, 0.0).astype(bf16)
        for o in range(RING):
            facts = xa[0, zz * RING + o, pl.ds(OWN, INFO), pl.ds(0, OWN)].astype(f32)
            named, values = facts[0:8], facts[8:16]
            found = [
                jnp.sum(jnp.where(named == (me * HELD + j).astype(f32), values, 0.0), axis=0, keepdims=True)
                for j in range(HELD)
            ]
            held = jnp.concatenate(found + [jnp.zeros((8 - HELD, OWN), f32)], axis=0).astype(bf16)
            gx[pl.ds(o * OWN, OWN)] = lax.dot_general(
                held, expand, (((0,), (0,)), ((), ())), preferred_element_type=f32
            ).astype(bf16)

    @scoped("hidden")
    def hidden(zz, i):
        units = pl.ds(i * TILE, TILE)
        gate = jnp.zeros((BATCH, TILE), f32)
        up = jnp.zeros((BATCH, TILE), f32)
        for half in range(2):
            for kind in range(2):
                block = bufs[kind][half, pl.ds(zz * RING, RING), pl.ds(0, OWN)].reshape(BATCH, QUART)
                columns = pl.ds(half * 2048 + kind * QUART, QUART)
                gate = gate + lax.dot_general(block, wg[units, columns], NT, preferred_element_type=f32)
                up = up + lax.dot_general(block, wu[units, columns], NT, preferred_element_type=f32)
        scale = gx[:, units].astype(f32)
        hid[:, units] = (gate * (1.0 / (1.0 + jnp.exp(-gate))) * up * scale).astype(bf16)

    def d_copy(s, i):
        return pltpu.make_async_remote_copy(
            src_ref=theirs.at[s, i], dst_ref=dgot.at[s, i], send_sem=d_s.at[s, i], recv_sem=d_r.at[s, i],
            device_id=device(0, 0, 0, other), device_id_type=MESH,
        )

    def down(i, core):
        column = pl.multiple_of((((y + ORDER[i]) % RING) * 2 + core) * CHUNK, CHUNK)
        return jnp.dot(hid[...], wd[:, pl.ds(column, CHUNK)], preferred_element_type=f32).astype(bf16)

    def backs(b, hook):
        s = b % 2

        def ours(i):
            with jax.named_scope("ours"):
                mine[b % 3, i] = down(i, c)

        def yours(i):
            with jax.named_scope("yours"):
                theirs[s, i] = down(i, other)
                d_copy(s, i).start()

        def join(i):
            with jax.named_scope("join"):
                d_copy(s, i).wait()
            mine[b % 3, i] = (mine[b % 3, i].astype(f32) + dgot[s, i].astype(f32)).astype(bf16)

        yours(0)
        yours(1)
        ours(0)
        yours(2)
        join(0)
        hook(4)
        yours(3)
        ours(1)
        join(1)
        hook(5)
        ours(2)
        join(2)
        hook(6)
        ours(3)
        join(3)
        hook(7)

    with jax.named_scope("enter"):
        pl.semaphore_wait(barrier, len(peers))
    with jax.named_scope("own"):
        finish(own_loads)
    spread(0, True, 0, 0)
    spread(1, True, 0, 0)
    spread(1, False, 0, 0)
    spread(0, False, 0, 0)

    with jax.named_scope("first"):
        arrive(0, True, 0, 3)
        arrive(0, True, 0, 1)
        arrive(1, True, 3, 0)
        arrive(1, True, 1, 0)
    with jax.named_scope("second"):
        arrive(1, False, 0, 3)
        arrive(1, False, 0, 1)
        spread(1, False, 1, 0)
        spread(1, False, 3, 0)
        spread(0, False, 0, 3)
        spread(0, False, 0, 1)
        arrive(0, True, 0, 2)
        spread(0, False, 0, 2)
    with jax.named_scope("opposite"):
        arrive(1, False, 0, 2)
        pairs(0)
    finish(weight_loads)

    def a(dz, dx):
        return lambda: arrive(0, False, dz, dx)

    def bb(dz, dx):
        return lambda: arrive(1, dx == 0, dz, dx)

    def run(f, *args):
        return lambda: f(*args)

    plan = {
        (0, 0): [a(1, 0), a(3, 0)],
        (0, 1): [a(3, 3), a(1, 3)],
        (0, 2): [bb(1, 3), bb(1, 1)],
        (0, 3): [a(3, 1), a(1, 1)],
        (0, 4): [run(y_first, 0)],
        (0, 5): [bb(2, 0)],
        (0, 7): [bb(3, 3), bb(3, 1), run(spread, 1, False, 2, 0)],
        (1, 0): [a(1, 2), a(3, 2), bb(1, 2), run(pairs, 1), run(y_second, 0)],
        (1, 1): [bb(3, 2)],
        (1, 3): [bb(2, 3), bb(2, 1)],
        (1, 4): [run(y_first, 1)],
        (1, 7): [run(x_first, 1)],
        (2, 0): [run(pairs, 3)],
        (2, 1): [a(2, 0), a(2, 3), a(2, 1), a(2, 2), bb(2, 2)],
        (2, 2): [run(y_third, 0), run(x_second, 1)],
        (2, 3): [run(y_second, 1)],
        (2, 4): [run(y_first, 2)],
        (2, 7): [run(x_first, 2), run(y_final, 0)],
        (3, 0): [run(pairs, 2)],
        (3, 1): [run(x_third, 1), run(y_third, 1)],
        (3, 2): [run(x_second, 2), run(y_second, 2)],
        (3, 3): [run(x_final, 1), run(y_final, 1)],
        (3, 4): [run(y_first, 3)],
        (3, 7): [run(x_first, 3), run(x_third, 2), run(y_third, 2)],
    }

    def batch(b, carry):
        def hook(point):
            for value in range(RING):
                work = plan.get((value, point), [])
                if work:

                    @pl.when(b == value)
                    def _():
                        with jax.named_scope("hook%d" % point):
                            for item in work:
                                item()

        zz = (z + batch_z(b)) % RING
        hook(0)
        gates(zz)
        for i in range(HID // TILE):
            hidden(zz, i)
            hook(1 + i)
        backs(b, hook)
        return carry

    lax.fori_loop(0, RING, batch, 0)
    y_second(3)
    x_second(3)
    y_final(2)
    x_final(2)
    y_third(3)
    x_third(3)
    y_final(3)
    x_final(3)
    with jax.named_scope("last"):
        sums = []
        for part, ref in enumerate((zy, zx)):
            total = kept[:, pl.ds(part * LANES, LANES)]
            for b in range(1, RING):
                z_copy(b, part).wait()
                total = total + ref[b - 1].astype(f32)
            out[:, pl.ds(part * LANES, LANES)] = total.astype(bf16)
    with jax.named_scope("leave"):
        for describe_one, args in started:
            describe_one(*args).wait_send()


def gate_of(scores):
    lifted = jnp.exp(scores)
    return (lifted / jnp.sum(lifted, axis=-1, keepdims=True)).astype(bf16)


def local(tokens, scores, expert_ids, gate_weight, up_weight, down_weight):
    info = jnp.concatenate([expert_ids.astype(bf16).T, gate_of(scores).T], axis=0)
    info = jnp.pad(info, ((0, 0), (0, QUART - OWN)))
    weights = [w.reshape(HID, WIDTH) for w in (gate_weight, up_weight, down_weight)]
    dma = pltpu.SemaphoreType.DMA
    count = len(IDS)
    scratch = [
        (2, 16, OWN + INFO, QUART), (2, 16, OWN, QUART),
        (HID, WIDTH), (HID, WIDTH), (HID, WIDTH),
        (BATCH, HID), (BATCH, HID),
        (3, 4, BATCH, CHUNK), (2, 4, BATCH, CHUNK), (2, 4, BATCH, CHUNK),
        (2, 256, CHUNK), (3, 2, 256, LANES),
        (2, BATCH, CHUNK), (3, 2, BATCH, LANES),
        (BATCH, CHUNK), (3, BATCH, LANES),
        (3, OWN, CHUNK), (3, 3, OWN, LANES),
        (3, 2, 4, 64, LANES), (3, 2, 4, OWN, LANES),
        (3, 4, OWN, LANES), (3, 3, OWN, LANES),
    ]
    return pl.pallas_call(
        kernel,
        out_shape=jax.ShapeDtypeStruct((OWN, CHUNK), bf16),
        in_specs=[pl.BlockSpec(memory_space=pl.ANY)] * 5,
        out_specs=pl.BlockSpec(memory_space=pltpu.VMEM),
        scratch_shapes=[pltpu.VMEM(shape, bf16) for shape in scratch]
        + [pltpu.VMEM((OWN, CHUNK), f32)]
        + [pltpu.VMEM((3, OWN, LANES), bf16)] * 4
        + [dma((9,)), dma((count,)), dma((count,)), dma((2, 4)), dma((2, 4)), dma((64,)), dma((64,))],
        compiler_params=pltpu.CompilerParams(
            collective_id=0, has_side_effects=True, vmem_limit_bytes=67043328
        ),
    )(tokens, info, *weights)


def solution(mesh):
    in_specs = (
        P("expert", None),
        P("expert", None),
        P("expert", None),
        P("expert", "tensor", None),
        P("expert", "tensor", None),
        P("expert", "tensor", None),
    )
    out_specs = P("expert", "tensor")
    return jax.shard_map(local, mesh=mesh, in_specs=in_specs, out_specs=out_specs, check_vma=False)
```

time: 371 us -> 124 us (0.33)
  Pallas kernels: 0 us -> 119 us
  waiting for transfers between devices: 105 us -> 0 us
  local copies, waits for them, and re-layouts: 86.3 us -> 1.57 us
  blocking collectives: 71 us -> 0 us
  other arithmetic: 50.3 us -> 2.71 us
  matrix products: 32.6 us -> 0 us
  between operations: 13.7 us -> 0.01 us
  starting transfers between devices: 10.5 us -> 0 us
    pallas_call x0 -> x1, Pallas kernels: none -> 119 us  [local(): pl.pallas_call(kernel, out_shape=jax.ShapeDtypeStruct((OWN, CHUNK), bf16)...]
    all_gather x1 -> x0, waiting for transfers between devices: 82.7 us -> none  [local(): piece = lax.all_gather(arrived, 'tensor', axis=2, tiled=True)]
    all_to_all x2 -> x0, blocking collectives: 71 us -> none  [the longest x1 36.2 us: local(): lax.all_to_all(outgoing, 'expert', split_axis=1, concat_axis=1, tiled=True)]
    unnamed x24 -> x1, local copies, waits for them, and re-layouts: 62.8 us -> 1.57 us
    dot_general x2 -> x0, matrix products: 32.6 us -> none  [the longest x1 21.6 us: local(): jnp.einsum('jcf,jfd->jcd', hidden, down_weight, preferred_element_type=jn...]
    another operation x2 -> x0, other arithmetic: 27.8 us -> none  [slot_tables(): rank_in_block = jnp.cumsum(folded, axis=1) - folded]
    all_to_all x2 -> x0, waiting for transfers between devices: 15.1 us -> none  [copy_for_each(): return lax.all_to_all(copies, axis, split_axis=0, concat_axis=0, tiled=True)]
    scatter-add x1 -> x0, other arithmetic: 12.9 us -> none  [local(): mixed = jnp.zeros((owner_rows, share), jnp.float32).at[send_index].add(re...]
  transfers between devices with their start and end apart: 4 -> 0, of which waited for: 4 -> 0; matrix products, arithmetic and copies ran while one was open for 16% -> 0% of each run, Pallas kernels for 0% -> 0%
where the time goes in v2:
time: 124 us; the launch traced here: 123 us
  Pallas kernels  119 us (96%)
  other arithmetic  2.71 us (2%)
  local copies, waits for them, and re-layouts  1.57 us (1%)
    pallas_call x1, Pallas kernels, local(): pl.pallas_call(kernel, out_shape=jax.ShapeDtypeStruct((OWN, CHUNK), bf16)...  119 us

profile of v2, /device:TPU:0, one launch (start us, length us, event | category | flops | bytes accessed | tf_op | source)
XLA Modules:
  0.0 123.4 jit_solution(18141879727846209141)
XLA Ops:
  0.0 0.7 exponential_reduce_fusion
  0.7 0.7 fusion.3
  1.4 0.7 convert_bitcast_fusion
  2.1 0.6 fusion.2.info
  2.7 119.1 %shard_map.64 = bf16[128,512]{1,0:T(8,128)(2,1)} custom-call(bf16[128,4096]{1,0:T(8,128)(2,1)} %tokens.1, bf16[16,1024]{1,0:T(8,128)(2,1)} %fusion.2.info, bf16[768,4096]{1,0:T(8,128)(2,1)} %bitcast.7, bf16[768,4096]{1,0:T(8,128)(2,1)} %bitcast.8, bf16[768,4096]{1,0:T(8,128)(2,1)} %bitcast.9), custom_call_target="tpu_custom_call" | custom-call | tf_op jit(solution)/shard_map/pallas_call | solution.py:522
  121.9 1.6 %copy.8 = bf16[128,512]{1,0:T(8,128)(2,1)} copy(bf16[128,512]{1,0:T(8,128)(2,1)} %shard_map.64) | data formatting | bytes 262144

commit v3 on v2

v3 whole, which is shorter than its diff:
```python
import jax
import jax.numpy as jnp
from jax import lax
from jax.experimental import pallas as pl
from jax.experimental.pallas import tpu as pltpu
from jax.sharding import PartitionSpec as P

MESH = pl.DeviceIdType.MESH
f32 = jnp.float32
bf16 = jnp.bfloat16

RING = 4
OWN = 128
WIDTH = 4096
FFS = 192
HELD = 4
QUART = 1024
INFO = 16
CHUNK = 512
TOP = 8
HID = HELD * FFS
TILE = 256
LANES = 256
HALF = OWN // 2
STEPS = 2 * RING
BATCH = RING * HALF
ORDER = (2, 1, 3, 0)
NT = (((1,), (1,)), ((), ()))


def distance(kind, dz, dx):
    if kind == 0:
        return dx if dz == 0 else dz
    return dz if dx == 0 else dx


def transfer_ids():
    ids = {}
    for kind in range(2):
        for dz in range(RING):
            for dx in range(RING):
                if dz == 0:
                    continue
                ids[kind, dz, dx] = len(ids)
    for dz in range(RING):
        ids[dz] = len(ids)
    return ids


IDS = transfer_ids()


def scoped(name):
    def wrap(body):
        def inner(*args):
            with jax.named_scope(name):
                return body(*args)

        return inner

    return wrap


def kernel(
    tokens, scores, ids, wg_in, wu_in, wd_in, out,
    xall, facts, score_buf, ids_buf, wg, wu, wd, hid, gx, mine, chunk, dgot,
    y1a, y1b, y2a, y2b, tota, totb, xs1a, xs1b, xs2a, xs2b, xs3, xg1, xg2, wrow, ys1, ys2, ys3, kept, leave_y, leave_x, zy, zx,
    lsem, gsem, rsem, d_s, d_r, q_s, q_r,
):
    me = lax.axis_index("expert")
    rank = lax.axis_index("tensor")
    z, x = me // RING, me % RING
    y, c = rank // 2, rank % 2
    other = 1 - c

    def device(dz, dx, dy, core):
        return (((z + dz) % RING) * RING + (x + dx) % RING, ((y + dy) % RING) * 2 + core)

    peers = [device(0, 0, 0, other)]
    for step in (1, 3, 2):
        peers += [device(0, step, 0, c), device(step, 0, 0, c)]
    peers += [device(0, 0, step, c) for step in (1, 3, 2)]
    barrier = pltpu.get_barrier_semaphore()
    for peer in peers:
        pl.semaphore_signal(barrier, inc=1, device_id=peer, device_id_type=MESH)

    loads = []

    def load(src, dst):
        copy = pltpu.make_async_copy(src, dst, lsem.at[len(loads)])
        loads.append(copy)
        copy.start()
        return copy

    fact_loads = [load(scores, score_buf), load(ids, ids_buf)]
    own_loads = []
    for half in range(2):
        for kind in range(2):
            own_loads.append(
                load(tokens.at[:, pl.ds(half * 2048 + kind * QUART, QUART)], xall.at[kind, half, me])
            )

    def view(kind, half, dz, dx, part):
        owner = ((z + dz) % RING) * RING + (x + dx) % RING
        if part == "h0":
            return xall.at[kind, half, owner, pl.ds(0, 64)]
        if part == "h1":
            return xall.at[kind, half, owner, pl.ds(64, 64)]
        return xall.at[kind, half, owner]

    sent = {}

    def push(key, ref, to, ident, group=0):
        copy = pltpu.make_async_remote_copy(
            src_ref=ref, dst_ref=ref, send_sem=gsem.at[group], recv_sem=rsem.at[ident],
            device_id=to, device_id_type=MESH,
        )
        sent[key] = ref.size
        copy.start()

    def pull(ref, ident):
        pltpu.make_async_remote_copy(
            src_ref=ref, dst_ref=ref, send_sem=gsem.at[0], recv_sem=rsem.at[ident],
            device_id=device(0, 0, 0, other), device_id_type=MESH,
        ).wait_recv()

    def send(kind, dz, dx, part, tz, tx):
        ident = IDS[kind, (dz - tz) % RING, (dx - tx) % RING]
        push((kind, dz, dx, part, tz, tx), view(kind, c, dz, dx, part), device(tz, tx, 0, c), ident)

    def pair(kind, dz, dx):
        push((kind, dz, dx), view(kind, c, dz, dx, "f"), device(0, 0, 0, other), IDS[dz])

    def pairs(dz):
        count = RING if dz else RING - 1
        pull(xall.at[:, other, pl.ds(0, count)], IDS[dz])

    def along(kind, first, step):
        if (kind == 0) == first:
            return (0, step)
        return (step, 0)

    def arrive(kind, first, dz, dx):
        d = distance(kind, dz, dx)
        pull(view(kind, c, dz, dx, "f"), IDS[kind, dz, dx])
        if d != 2:
            if d == 3:
                send(kind, dz, dx, "h0", *along(kind, first, 1))
            else:
                send(kind, dz, dx, "h1", *along(kind, first, 3))
        pair(kind, dz, dx)

    def spread(kind, first, dz, dx):
        for step in (1, 3):
            send(kind, dz, dx, "f", *along(kind, first, step))

    queue_ids = {}

    def queued(key, src, dst, to):
        ident = queue_ids.setdefault(key, len(queue_ids))
        return pltpu.make_async_remote_copy(
            src_ref=src, dst_ref=dst, send_sem=q_s.at[ident], recv_sem=q_r.at[ident],
            device_id=to, device_id_type=MESH,
        )

    def begin(copies):
        for copy in copies:
            copy.start()

    def finish(copies):
        for copy in copies:
            copy.wait()

    def batch_z(b):
        return (b * (b + 1) // 2) % RING

    def wide(b):
        return CHUNK if b < 2 else LANES

    def y1(b):
        return y1a.at[b] if b < 2 else y1b.at[b - 2]

    def y2(b):
        return y2a.at[b] if b < 2 else y2b.at[b - 2]

    def tot(b):
        return tota.at[b] if b < 2 else totb.at[b - 2]

    def xs1(b):
        return xs1a.at[b] if b < 2 else xs1b.at[b - 2]

    def xs2(b):
        return xs2a.at[b] if b < 2 else xs2b.at[b - 2]

    def owner_rows(dx, start, size):
        return pl.ds(pl.multiple_of(((x + dx) % RING) * HALF + start, 32), size)

    def y_copies(b, stage):
        lanes = pl.ds(0, wide(b))
        if stage == 0:
            pieces = [(mine.at[b % 4, 0, pl.ds(n * 128, 128), lanes], y1(b).at[n]) for n in range(2)]
        else:
            pieces = [(mine.at[b % 4, 1 + n, :, lanes], y2(b).at[n]) for n in range(2)]
        return [
            queued(("y", b if b < 2 else 2 + b % 2, stage, n), src, dst, device(0, 0, (1, 3)[n], c)) for n, (src, dst) in enumerate(pieces)
        ]

    def direct(b):
        return b == STEPS - 1

    def y_last(b, stage):
        if direct(b):
            return [
                queued(("ydirect", d), tot(b).at[owner_rows(d, 0, HALF)], xs3.at[d - 1], device(0, d, 0, c))
                for d in (2, 1, 3)
            ]
        if stage == 0:
            pieces = [(tot(b).at[owner_rows(2, 32 * n, 32)], xs1(b).at[n]) for n in range(2)]
        else:
            pieces = [(tot(b).at[owner_rows((1, 3)[n], 0, HALF)], xs2(b).at[n]) for n in range(2)]
        return [
            queued(("ylast", b if b < 2 else 2 + b % 2, stage, n), src, dst, device(0, (1, 3)[n], 0, c)) for n, (src, dst) in enumerate(pieces)
        ]

    @scoped("y_first")
    def y_first(b):
        begin(y_copies(b, 0))

    @scoped("y_second")
    def y_second(b):
        finish(y_copies(b, 0))
        lanes = pl.ds(0, wide(b))
        for n in range(2):
            rows = pl.ds(n * 128, 128)
            mine[b % 4, 1 + n, rows, lanes] = (
                mine[b % 4, 1 + n, rows, lanes].astype(f32) + y1(b)[n].astype(f32)
            ).astype(bf16)
        begin(y_copies(b, 1))

    @scoped("y_third")
    def y_third(b):
        finish(y_copies(b, 1))
        tot(b)[...] = (
            mine[b % 4, 3, :, pl.ds(0, wide(b))].astype(f32) + y2(b)[0].astype(f32) + y2(b)[1].astype(f32)
        ).astype(bf16)
        begin(y_last(b, 0))

    @scoped("y_mid")
    def y_mid(b):
        finish(y_last(b, 0))
        for n in range(2):
            rows = owner_rows((1, 3)[n], 32 * n, 32)
            tot(b)[rows] = (tot(b)[rows].astype(f32) + xs1(b)[n].astype(f32)).astype(bf16)
        begin(y_last(b, 1))

    def z_copy(b, part):
        src, dst = ((leave_y, zy), (leave_x, zx))[part]
        return queued(("z", b, part), src.at[b - 2], dst.at[b - 2], device(batch_z(b // 2), 0, 0, c))

    @scoped("y_final")
    def y_final(b):
        finish(y_last(b, 1))
        value = tot(b)[owner_rows(0, 0, HALF)].astype(f32)
        for ref in [xs3.at[n] for n in range(3)] if direct(b) else [xs2(b).at[n] for n in range(2)]:
            value = value + ref[...].astype(f32)
        if b < 2:
            kept[pl.ds(b * HALF, HALF)] = value
        else:
            leave_y[b - 2] = value.astype(bf16)
            z_copy(b, 0).start()

    upper = pl.ds(LANES, LANES)

    def x_copies(b, stage, p):
        both = pl.ds(2 * p, 2)
        if stage == 0:
            pieces = [
                (mine.at[b % 4, both, owner_rows(2, 32 * n, 32), upper], xg1.at[b - 2, n, both]) for n in range(2)
            ]
        else:
            pieces = [
                (mine.at[b % 4, both, owner_rows((1, 3)[n], 0, HALF), upper], xg2.at[b - 2, n, both])
                for n in range(2)
            ]
        return [
            queued(("x", b % 2, stage, n, p), src, dst, device(0, (1, 3)[n], 0, c))
            for n, (src, dst) in enumerate(pieces)
        ]

    def x_last(b, stage):
        if direct(b):
            return [
                queued(("xdirect", i), wrow.at[b - 2, i], ys3.at[i], device(0, 0, ORDER[i], c)) for i in range(3)
            ]
        if stage == 0:
            pieces = [(wrow.at[b - 2, 0, pl.ds(32 * n, 32)], ys1.at[b - 2, n]) for n in range(2)]
        else:
            pieces = [(wrow.at[b - 2, 1 + n], ys2.at[b - 2, n]) for n in range(2)]
        return [
            queued(("xlast", b % 2, stage, n), src, dst, device(0, 0, (1, 3)[n], c)) for n, (src, dst) in enumerate(pieces)
        ]

    @scoped("x_first")
    def x_first(b, p):
        begin(x_copies(b, 0, p))

    @scoped("x_second")
    def x_second(b):
        for p in range(2):
            finish(x_copies(b, 0, p))
            for n in range(2):
                rows = owner_rows((1, 3)[n], 32 * n, 32)
                for i in (2 * p, 2 * p + 1):
                    mine[b % 4, i, rows, upper] = (
                        mine[b % 4, i, rows, upper].astype(f32) + xg1[b - 2, n, i].astype(f32)
                    ).astype(bf16)
            begin(x_copies(b, 1, p))

    @scoped("x_third")
    def x_third(b):
        rows = owner_rows(0, 0, HALF)
        for p in range(2):
            finish(x_copies(b, 1, p))
            for i in (2 * p, 2 * p + 1):
                wrow[b - 2, i] = (
                    mine[b % 4, i, rows, upper].astype(f32)
                    + xg2[b - 2, 0, i].astype(f32)
                    + xg2[b - 2, 1, i].astype(f32)
                ).astype(bf16)
            if p == direct(b):
                begin(x_last(b, 0))

    @scoped("x_mid")
    def x_mid(b):
        finish(x_last(b, 0))
        for n in range(2):
            rows = pl.ds(32 * n, 32)
            wrow[b - 2, 1 + n, rows] = (
                wrow[b - 2, 1 + n, rows].astype(f32) + ys1[b - 2, n].astype(f32)
            ).astype(bf16)
        begin(x_last(b, 1))

    @scoped("x_final")
    def x_final(b):
        finish(x_last(b, 1))
        value = wrow[b - 2, 3].astype(f32)
        for ref in [ys3.at[n] for n in range(3)] if direct(b) else [ys2.at[b - 2, n] for n in range(2)]:
            value = value + ref[...].astype(f32)
        leave_x[b - 2] = value.astype(bf16)
        z_copy(b, 1).start()

    @scoped("gates")
    def gates(zz):
        member = lax.broadcasted_iota(jnp.int32, (8, HID), 0)
        unit = lax.broadcasted_iota(jnp.int32, (8, HID), 1)
        expand = jnp.where((unit >= member * FFS) & (unit < member * FFS + FFS), 1.0, 0.0).astype(bf16)
        for o in range(RING):
            about = facts[zz * RING + o].astype(f32)
            named, values = about[0:8], about[8:16]
            found = [
                jnp.sum(jnp.where(named == (me * HELD + j).astype(f32), values, 0.0), axis=0, keepdims=True)
                for j in range(HELD)
            ]
            held = jnp.concatenate(found + [jnp.zeros((8 - HELD, OWN), f32)], axis=0).astype(bf16)
            gx[zz * RING + o] = lax.dot_general(
                held, expand, (((0,), (0,)), ((), ())), preferred_element_type=f32
            ).astype(bf16)

    @scoped("hidden")
    def hidden(zz, rows, i):
        units = pl.ds(i * TILE, TILE)
        gate = jnp.zeros((BATCH, TILE), f32)
        up = jnp.zeros((BATCH, TILE), f32)
        for half in range(2):
            for kind in range(2):
                block = xall[kind, half, pl.ds(zz * RING, RING), rows].reshape(BATCH, QUART)
                columns = pl.ds(half * 2048 + kind * QUART, QUART)
                gate = gate + lax.dot_general(block, wg[units, columns], NT, preferred_element_type=f32)
                up = up + lax.dot_general(block, wu[units, columns], NT, preferred_element_type=f32)
        scale = gx[pl.ds(zz * RING, RING), rows, units].reshape(BATCH, TILE).astype(f32)
        hid[:, units] = (gate * (1.0 / (1.0 + jnp.exp(-gate))) * up * scale).astype(bf16)

    def d_copy(s, i):
        return pltpu.make_async_remote_copy(
            src_ref=chunk.at[i, other], dst_ref=dgot.at[s, i], send_sem=d_s.at[s, i], recv_sem=d_r.at[s, i],
            device_id=device(0, 0, 0, other), device_id_type=MESH,
        )

    def down(s, i):
        with jax.named_scope("down"):
            column = pl.multiple_of(((y + ORDER[i]) % RING) * 2 * CHUNK, CHUNK)
            value = jnp.dot(hid[...], wd[:, pl.ds(column, 2 * CHUNK)], preferred_element_type=f32).astype(bf16)
            chunk[i, 0] = value[:, :CHUNK]
            chunk[i, 1] = value[:, CHUNK:]
            d_copy(s, i).start()

    def join(b, s, i):
        with jax.named_scope("join"):
            d_copy(s, i).wait()
        mine[b % 4, i] = (chunk[i, c].astype(f32) + dgot[s, i].astype(f32)).astype(bf16)

    def backs(b, hook):
        s = b % 2
        down(s, 0)
        down(s, 1)
        down(s, 2)
        join(b, s, 0)
        hook(4)
        down(s, 3)
        join(b, s, 1)
        hook(5)
        join(b, s, 2)
        hook(6)

    def fact_copies(stage):
        if stage == 0:
            for d in (2, 1, 3):
                push(("fx", d), facts.at[me], device(0, d, 0, c), len(IDS), 1)
        else:
            for d in (2, 1, 3):
                push(("fz", d), facts.at[pl.ds(z * RING, RING)], device(d, 0, 0, c), len(IDS) + 1, 1)

    def fact_waits(stage):
        pull(facts.at[pl.ds(0, 12 if stage else 3)], len(IDS) + stage)

    finish(fact_loads)
    lifted = jnp.exp(score_buf[...])
    gate_values = (lifted / jnp.sum(lifted, axis=0, keepdims=True)).astype(bf16).astype(f32)
    facts[me] = jnp.concatenate([ids_buf[...].astype(f32), gate_values], axis=0).astype(bf16)

    with jax.named_scope("enter"):
        pl.semaphore_wait(barrier, len(peers))
    with jax.named_scope("own"):
        finish(own_loads)
    parity = y % 2

    def own_view(dx, h, lanes):
        owner = z * RING + (x + dx) % RING
        rows = pl.ds(0, OWN) if h is None else pl.ds(64 * h, 64)
        return xall.at[:, c, owner, rows, pl.ds(pl.multiple_of(lanes * CHUNK, CHUNK), CHUNK)]

    own_ids = {}

    def own_send(axis, dx, h, step):
        key = ("x", (dx - step) % RING, h) if axis == "x" else ("y", dx)
        ident = own_ids.setdefault(key, len(IDS) + 2 + len(own_ids))
        to = device(0, step, 0, c) if axis == "x" else device(0, 0, step, c)
        push((axis, dx, h, step), own_view(dx, h, parity), to, ident)

    def own_got(axis, dx, h):
        if axis == "x":
            pull(own_view(dx, h, parity), own_ids["x", dx, h])
        else:
            pull(own_view(dx, None, 1 - parity), own_ids["y", dx])

    def sideways(dx, h):
        own_send("y", dx, h, (1, 3)[h])

    fact_copies(0)
    own_send("x", 0, 0, 1)
    own_send("x", 0, 1, 3)
    own_send("x", 0, 1, 1)
    own_send("x", 0, 0, 3)
    spread(1, True, 0, 0)
    fact_waits(0)
    fact_copies(1)
    spread(0, False, 0, 0)

    weight_loads = [load(wg_in, wg), load(wu_in, wu), load(wd_in, wd)]
    with jax.named_scope("ox1"):
        own_got("x", 3, 0)
        own_send("x", 3, 0, 1)
        sideways(3, 0)
        own_got("x", 1, 1)
        own_send("x", 1, 1, 3)
        sideways(1, 1)
    with jax.named_scope("ox2"):
        own_got("x", 3, 1)
        sideways(3, 1)
        own_got("x", 1, 0)
        sideways(1, 0)
    with jax.named_scope("bz"):
        arrive(1, True, 3, 0)
        arrive(1, True, 1, 0)
    with jax.named_scope("ox3"):
        own_got("x", 2, 0)
        sideways(2, 0)
        own_got("x", 2, 1)
        sideways(2, 1)
        spread(1, False, 1, 0)
        spread(1, False, 3, 0)
    gates(z)
    with jax.named_scope("fz"):
        fact_waits(1)
    gates((z + 1) % RING)
    gates((z + 2) % RING)
    for dx in (3, 1, 2):
        with jax.named_scope("oy%d" % dx):
            own_got("y", dx, 0)
            spread(0, False, 0, dx)
            pair(0, 0, dx)
            pair(1, 0, dx)
        if dx == 1:
            gates((z + 3) % RING)
    with jax.named_scope("pairs"):
        pairs(0)
    finish(weight_loads)

    def a(dz, dx):
        return lambda: arrive(0, False, dz, dx)

    def bb(dz, dx):
        return lambda: arrive(1, dx == 0, dz, dx)

    def run(f, *args):
        return lambda: f(*args)

    def xf(b, i):
        return run(x_first, b, i)

    plan = {
        (0, 0): [a(1, 0), a(3, 0)],
        (0, 1): [bb(1, 3), bb(1, 1)],
        (0, 5): [a(3, 3), a(1, 3)],
        (1, 0): [bb(3, 3), bb(3, 1), bb(2, 0), run(spread, 1, False, 2, 0)],
        (1, 2): [a(3, 1), a(1, 1)],
        (2, 0): [a(1, 2), a(3, 2), bb(1, 2), bb(3, 2), run(pairs, 1)],
        (3, 0): [bb(2, 3), bb(2, 1)],
        (4, 0): [run(pairs, 3)],
        (4, 1): [a(2, 0), a(2, 3), a(2, 1), bb(2, 2), a(2, 2)],
        (6, 0): [run(pairs, 2)],
    }

    def later(step, point, work):
        plan.setdefault((step, point), []).append(work)

    for b in range(STEPS):
        later(b, 4, run(y_first, b))
        if b > 1:
            later(b, 5, run(x_first, b, 0))
            later(b + 1, 1, run(x_first, b, 1))
    for step in range(STEPS):
        for lag, point, work in (
            (3, 1, x_mid), (3, 1, y_mid), (2, 3, y_third), (2, 3, x_third),
            (1, 3, y_second), (1, 4, x_second), (3, 6, y_final), (3, 6, x_final),
        ):
            if step - lag > 1:
                later(step, point, run(work, step - lag))
    for b in range(2):
        later(b + 1, 4, run(y_second, b))
        later(b + 3, 1, run(y_third, b))
        later(b + 4, 1, run(y_mid, b))
        later(b + 5, 1, run(y_final, b))

    def batch(b, carry):
        def hook(point):
            for value in range(STEPS):
                work = plan.get((value, point), [])
                if work:

                    @pl.when(b == value)
                    def _():
                        with jax.named_scope("hook%d" % point):
                            for item in work:
                                item()

        zz = (z + batch_z(b // 2)) % RING
        rows = pl.ds(pl.multiple_of((b % 2) * HALF, HALF), HALF)
        hook(0)
        for i in range(HID // TILE):
            hidden(zz, rows, i)
            if i == 0:

                @pl.when(b > 0)
                def _():
                    join(b + 3, (b + 1) % 2, 3)

            hook(1 + i)
        backs(b, hook)
        return carry

    lax.fori_loop(0, STEPS, batch, 0)
    join(STEPS - 1, (STEPS - 1) % 2, 3)
    final = STEPS - 1
    x_first(final, 1)
    x_mid(final - 2)
    y_mid(final - 2)
    y_second(final)
    x_second(final)
    y_third(final - 1)
    x_third(final - 1)
    y_final(final - 2)
    x_final(final - 2)
    y_mid(final - 1)
    x_mid(final - 1)
    y_third(final)
    x_third(final)
    for b in (final - 1, final):
        y_final(b)
        x_final(b)
    with jax.named_scope("last"):
        for part, ref in enumerate((zy, zx)):
            for h in range(2):
                rows, lanes = pl.ds(h * HALF, HALF), pl.ds(part * LANES, LANES)
                total = kept[rows, lanes]
                for b in range(2 + h, STEPS, 2):
                    z_copy(b, part).wait()
                    total = total + ref[b - 2].astype(f32)
                out[rows, lanes] = total.astype(bf16)
    with jax.named_scope("leave"):
        block = OWN * QUART
        small = sum(size for key, size in sent.items() if key[0] in ("fx", "fz"))
        blocks = (sum(sent.values()) - small) // block
        assert blocks * block + small == sum(sent.values())
        assert blocks == 60 and small == 15 * INFO * OWN
        for group, ref in enumerate((xall.at[:, :, pl.ds(0, 15)], facts.at[pl.ds(0, 15)])):
            pltpu.make_async_remote_copy(
                src_ref=ref, dst_ref=ref, send_sem=gsem.at[group], recv_sem=rsem.at[0],
                device_id=device(0, 0, 0, other), device_id_type=MESH,
            ).wait_send()


def local(tokens, scores, expert_ids, gate_weight, up_weight, down_weight):
    weights = [w.reshape(HID, WIDTH) for w in (gate_weight, up_weight, down_weight)]
    dma = pltpu.SemaphoreType.DMA
    count = len(IDS)
    scratch = [
        (HID, WIDTH), (HID, WIDTH), (HID, WIDTH),
        (BATCH, HID), (RING * RING, OWN, HID),
        (4, 4, BATCH, CHUNK), (4, 2, BATCH, CHUNK), (2, 4, BATCH, CHUNK),
        (2, 2, 128, CHUNK), (6, 2, 128, LANES),
        (2, 2, BATCH, CHUNK), (6, 2, BATCH, LANES),
        (2, BATCH, CHUNK), (6, BATCH, LANES),
        (2, 2, 32, CHUNK), (6, 2, 32, LANES), (2, 2, HALF, CHUNK), (6, 2, HALF, LANES), (3, HALF, LANES),
        (6, 2, 4, 32, LANES), (6, 2, 4, HALF, LANES),
        (6, 4, HALF, LANES), (6, 2, 32, LANES), (6, 2, HALF, LANES), (3, HALF, LANES),
    ]
    return pl.pallas_call(
        kernel,
        out_shape=jax.ShapeDtypeStruct((OWN, CHUNK), bf16),
        in_specs=[pl.BlockSpec(memory_space=pl.ANY)] * 6,
        out_specs=pl.BlockSpec(memory_space=pltpu.VMEM),
        scratch_shapes=[
            pltpu.VMEM((2, 2, 16, OWN, QUART), bf16), pltpu.VMEM((16, INFO, OWN), bf16),
            pltpu.VMEM((TOP, OWN), f32), pltpu.VMEM((TOP, OWN), jnp.int32),
        ]
        + [pltpu.VMEM(shape, bf16) for shape in scratch]
        + [pltpu.VMEM((OWN, CHUNK), f32)]
        + [pltpu.VMEM((6, HALF, LANES), bf16)] * 4
        + [dma((9,)), dma((2,)), dma((count + 11,)), dma((2, 4)), dma((2, 4)), dma((74,)), dma((74,))],
        compiler_params=pltpu.CompilerParams(
            collective_id=0, has_side_effects=True, vmem_limit_bytes=67043328
        ),
    )(tokens, scores.T, expert_ids.T, *weights)


def solution(mesh):
    in_specs = (
        P("expert", None),
        P("expert", None),
        P("expert", None),
        P("expert", "tensor", None),
        P("expert", "tensor", None),
        P("expert", "tensor", None),
    )
    out_specs = P("expert", "tensor")
    return jax.shard_map(local, mesh=mesh, in_specs=in_specs, out_specs=out_specs, check_vma=False)
```

time: 124 us -> 114 us (0.919)
  Pallas kernels: 119 us -> 112 us
  other arithmetic: 2.71 us -> 0 us
    pallas_call x1, Pallas kernels: 119 us -> 112 us  [local(): pl.pallas_call(kernel, out_shape=jax.ShapeDtypeStruct((OWN, CHUNK), bf16)...]
    transpose x2 -> x0, other arithmetic: 1.39 us -> none  [the longest x1 0.7 us: local(): gate_of(scores)]
where the time goes in v3:
time: 114 us
  Pallas kernels  112 us (98%)
  local copies, waits for them, and re-layouts  1.57 us (1%)
    pallas_call x1, Pallas kernels, local(): pl.pallas_call(kernel, out_shape=jax.ShapeDtypeStruct((OWN, CHUNK), bf16)...  112 us

profile of v3, /device:TPU:0, one launch (start us, length us, event | category | flops | bytes accessed | tf_op | source)
XLA Modules:
  0.0 113.5 jit_solution(10369449344514596632)
XLA Ops:
  0.0 112.0 %shard_map.64 = bf16[128,512]{1,0:T(8,128)(2,1)} custom-call(bf16[128,4096]{1,0:T(8,128)(2,1)} %tokens.1, f32[8,128]{1,0:T(8,128)} %bitcast.8, s32[8,128]{1,0:T(8,128)} %bitcast.9, bf16[768,4096]{1,0:T(8,128)(2,1)} %bitcast.5, bf16[768,4096]{1,0:T(8,128)(2,1)} %bitcast.6, bf16[768,4096]{1,0:T(8,128)(2,1)} %bitcast.7), custom_call_target="tpu_custom_call" | custom-call | tf_op jit(solution)/shard_map/pallas_call | solution.py:638
  112.0 1.6 %copy.8 = bf16[128,512]{1,0:T(8,128)(2,1)} copy(bf16[128,512]{1,0:T(8,128)(2,1)} %shard_map.64) | data formatting | bytes 262144

commit v4 on v3

--- a/solution.py
+++ b/solution.py
@@ -15,6 +15,7 @@
 FFS = 192
 HELD = 4
 QUART = 1024
+FIRST = 768
 INFO = 16
 CHUNK = 512
 TOP = 8
@@ -95,18 +96,13 @@
     fact_loads = [load(scores, score_buf), load(ids, ids_buf)]
     own_loads = []
     for half in range(2):
-        for kind in range(2):
-            own_loads.append(
-                load(tokens.at[:, pl.ds(half * 2048 + kind * QUART, QUART)], xall.at[kind, half, me])
-            )
+        own_loads.append(load(tokens.at[:, pl.ds(half * 2 * QUART, 2 * QUART)], xall.at[half, me]))
 
     def view(kind, half, dz, dx, part):
         owner = ((z + dz) % RING) * RING + (x + dx) % RING
-        if part == "h0":
-            return xall.at[kind, half, owner, pl.ds(0, 64)]
-        if part == "h1":
-            return xall.at[kind, half, owner, pl.ds(64, 64)]
-        return xall.at[kind, half, owner]
+        rows = {"h0": pl.ds(0, 64), "h1": pl.ds(64, 64), "f": pl.ds(0, OWN)}[part]
+        lanes = pl.ds(FIRST, 2 * QUART - FIRST) if kind else pl.ds(0, FIRST)
+        return xall.at[half, owner, rows, lanes]
 
     sent = {}
 
@@ -133,7 +129,7 @@
 
     def pairs(dz):
         count = RING if dz else RING - 1
-        pull(xall.at[:, other, pl.ds(0, count)], IDS[dz])
+        pull(xall.at[other, pl.ds(0, count)], IDS[dz])
 
     def along(kind, first, step):
         if (kind == 0) == first:
@@ -206,12 +202,12 @@
         ]
 
     def direct(b):
-        return b == STEPS - 1
+        return b >= STEPS - 3
 
     def y_last(b, stage):
         if direct(b):
             return [
-                queued(("ydirect", d), tot(b).at[owner_rows(d, 0, HALF)], xs3.at[d - 1], device(0, d, 0, c))
+                queued(("ydirect", b, d), tot(b).at[owner_rows(d, 0, HALF)], xs3.at[b - STEPS + 3, d - 1], device(0, d, 0, c))
                 for d in (2, 1, 3)
             ]
         if stage == 0:
@@ -261,7 +257,7 @@
     def y_final(b):
         finish(y_last(b, 1))
         value = tot(b)[owner_rows(0, 0, HALF)].astype(f32)
-        for ref in [xs3.at[n] for n in range(3)] if direct(b) else [xs2(b).at[n] for n in range(2)]:
+        for ref in [xs3.at[b - STEPS + 3, n] for n in range(3)] if direct(b) else [xs2(b).at[n] for n in range(2)]:
             value = value + ref[...].astype(f32)
         if b < 2:
             kept[pl.ds(b * HALF, HALF)] = value
@@ -283,14 +279,14 @@
                 for n in range(2)
             ]
         return [
-            queued(("x", b % 2, stage, n, p), src, dst, device(0, (1, 3)[n], 0, c))
+            queued(("x", b % 2 + b // (STEPS - 1), stage, n, p), src, dst, device(0, (1, 3)[n], 0, c))
             for n, (src, dst) in enumerate(pieces)
         ]
 
     def x_last(b, stage):
         if direct(b):
             return [
-                queued(("xdirect", i), wrow.at[b - 2, i], ys3.at[i], device(0, 0, ORDER[i], c)) for i in range(3)
+                queued(("xdirect", b, i), wrow.at[b - 2, i], ys3.at[b - STEPS + 3, i], device(0, 0, ORDER[i], c)) for i in range(3)
             ]
         if stage == 0:
             pieces = [(wrow.at[b - 2, 0, pl.ds(32 * n, 32)], ys1.at[b - 2, n]) for n in range(2)]
@@ -344,7 +340,7 @@
     def x_final(b):
         finish(x_last(b, 1))
         value = wrow[b - 2, 3].astype(f32)
-        for ref in [ys3.at[n] for n in range(3)] if direct(b) else [ys2.at[b - 2, n] for n in range(2)]:
+        for ref in [ys3.at[b - STEPS + 3, n] for n in range(3)] if direct(b) else [ys2.at[b - 2, n] for n in range(2)]:
             value = value + ref[...].astype(f32)
         leave_x[b - 2] = value.astype(bf16)
         z_copy(b, 1).start()
@@ -367,18 +363,40 @@
             ).astype(bf16)
 
     @scoped("hidden")
-    def hidden(zz, rows, i):
+    def hidden(load_block, load_scale, count, i):
         units = pl.ds(i * TILE, TILE)
-        gate = jnp.zeros((BATCH, TILE), f32)
-        up = jnp.zeros((BATCH, TILE), f32)
+        gate = jnp.zeros((count * OWN, TILE), f32)
+        up = jnp.zeros((count * OWN, TILE), f32)
         for half in range(2):
-            for kind in range(2):
-                block = xall[kind, half, pl.ds(zz * RING, RING), rows].reshape(BATCH, QUART)
-                columns = pl.ds(half * 2048 + kind * QUART, QUART)
+            for q in range(2):
+                block = load_block(half, pl.ds(q * QUART, QUART))
+                columns = pl.ds((half * 2 + q) * QUART, QUART)
                 gate = gate + lax.dot_general(block, wg[units, columns], NT, preferred_element_type=f32)
                 up = up + lax.dot_general(block, wu[units, columns], NT, preferred_element_type=f32)
-        scale = gx[pl.ds(zz * RING, RING), rows, units].reshape(BATCH, TILE).astype(f32)
-        hid[:, units] = (gate * (1.0 / (1.0 + jnp.exp(-gate))) * up * scale).astype(bf16)
+        scale = load_scale(units).astype(f32)
+        return (gate * (1.0 / (1.0 + jnp.exp(-gate))) * up * scale).astype(bf16)
+
+    def hidden_row(zz, i):
+        owners = pl.ds(zz * RING, RING)
+        value = hidden(
+            lambda half, lanes: xall[half, owners, :, lanes].reshape(RING * OWN, QUART),
+            lambda units: gx[owners, :, units].reshape(RING * OWN, TILE),
+            RING,
+            i,
+        )
+        hid[:, :, pl.ds(i * TILE, TILE)] = value.reshape(RING, OWN, TILE)
+
+    def hidden_owners(steps, i):
+        places = [(x + d) % RING for d in steps]
+        owners = [z * RING + place for place in places]
+        value = hidden(
+            lambda half, lanes: jnp.concatenate([xall[half, o, :, lanes] for o in owners], axis=0),
+            lambda units: jnp.concatenate([gx[o, :, units] for o in owners], axis=0),
+            len(owners),
+            i,
+        )
+        for n, place in enumerate(places):
+            hid[place, :, pl.ds(i * TILE, TILE)] = value[n * OWN : (n + 1) * OWN]
 
     def d_copy(s, i):
         return pltpu.make_async_remote_copy(
@@ -386,10 +404,10 @@
             device_id=device(0, 0, 0, other), device_id_type=MESH,
         )
 
-    def down(s, i):
+    def down(rows, s, i):
         with jax.named_scope("down"):
             column = pl.multiple_of(((y + ORDER[i]) % RING) * 2 * CHUNK, CHUNK)
-            value = jnp.dot(hid[...], wd[:, pl.ds(column, 2 * CHUNK)], preferred_element_type=f32).astype(bf16)
+            value = jnp.dot(hid[:, rows, :].reshape(BATCH, HID), wd[:, pl.ds(column, 2 * CHUNK)], preferred_element_type=f32).astype(bf16)
             chunk[i, 0] = value[:, :CHUNK]
             chunk[i, 1] = value[:, CHUNK:]
             d_copy(s, i).start()
@@ -399,14 +417,20 @@
             d_copy(s, i).wait()
         mine[b % 4, i] = (chunk[i, c].astype(f32) + dgot[s, i].astype(f32)).astype(bf16)
 
-    def backs(b, hook):
+    def backs(b, rows, hook):
         s = b % 2
-        down(s, 0)
-        down(s, 1)
-        down(s, 2)
+        down(rows, s, 0)
+
+        @pl.when(s == 1)
+        def _():
+            join(b + 3, 0, 3)
+
+        hook(3)
+        down(rows, s, 1)
+        down(rows, s, 2)
         join(b, s, 0)
         hook(4)
-        down(s, 3)
+        down(rows, s, 3)
         join(b, s, 1)
         hook(5)
         join(b, s, 2)
@@ -437,7 +461,7 @@
     def own_view(dx, h, lanes):
         owner = z * RING + (x + dx) % RING
         rows = pl.ds(0, OWN) if h is None else pl.ds(64 * h, 64)
-        return xall.at[:, c, owner, rows, pl.ds(pl.multiple_of(lanes * CHUNK, CHUNK), CHUNK)]
+        return xall.at[c, owner, rows, pl.ds(pl.multiple_of(lanes * QUART, QUART), QUART)]
 
     own_ids = {}
 
@@ -474,6 +498,9 @@
         own_got("x", 1, 1)
         own_send("x", 1, 1, 3)
         sideways(1, 1)
+    finish(weight_loads[:2])
+    gates(z)
+    hidden_owners((0,), 0)
     with jax.named_scope("ox2"):
         own_got("x", 3, 1)
         sideways(3, 1)
@@ -489,22 +516,21 @@
         sideways(2, 1)
         spread(1, False, 1, 0)
         spread(1, False, 3, 0)
-    gates(z)
     with jax.named_scope("fz"):
         fact_waits(1)
-    gates((z + 1) % RING)
-    gates((z + 2) % RING)
+    hidden_owners((0,), 1)
+    hidden_owners((0,), 2)
     for dx in (3, 1, 2):
         with jax.named_scope("oy%d" % dx):
             own_got("y", dx, 0)
             spread(0, False, 0, dx)
             pair(0, 0, dx)
             pair(1, 0, dx)
-        if dx == 1:
-            gates((z + 3) % RING)
+        if dx != 2:
+            gates((z + dx) % RING)
     with jax.named_scope("pairs"):
         pairs(0)
-    finish(weight_loads)
+    finish(weight_loads[2:])
 
     def a(dz, dx):
         return lambda: arrive(0, False, dz, dx)
@@ -520,37 +546,52 @@
 
     plan = {
         (0, 0): [a(1, 0), a(3, 0)],
-        (0, 1): [bb(1, 3), bb(1, 1)],
-        (0, 5): [a(3, 3), a(1, 3)],
-        (1, 0): [bb(3, 3), bb(3, 1), bb(2, 0), run(spread, 1, False, 2, 0)],
-        (1, 2): [a(3, 1), a(1, 1)],
-        (2, 0): [a(1, 2), a(3, 2), bb(1, 2), bb(3, 2), run(pairs, 1)],
-        (3, 0): [bb(2, 3), bb(2, 1)],
+        (0, 2): [bb(1, 3), bb(1, 1)],
+        (0, 4): [a(3, 3), a(1, 3)],
+        (1, 3): [a(3, 1), a(1, 1), bb(3, 3), bb(3, 1)],
+        (1, 4): [bb(2, 0), run(spread, 1, False, 2, 0)],
+        (2, 0): [run(gates, (z + 2) % RING), a(1, 2), a(3, 2), bb(1, 2), run(pairs, 1), run(y_second, 0)],
+        (2, 1): [run(y_second, 1)],
+        (2, 4): [run(y_third, 0)],
+        (3, 0): [bb(3, 2)],
+        (2, 6): [bb(2, 3), bb(2, 1)],
+        (3, 6): [run(y_mid, 0), run(y_third, 1)],
         (4, 0): [run(pairs, 3)],
-        (4, 1): [a(2, 0), a(2, 3), a(2, 1), bb(2, 2), a(2, 2)],
+        (4, 3): [a(2, 0), a(2, 3), a(2, 1), bb(2, 2), a(2, 2)],
+        (4, 2): [run(y_mid, 1), run(y_final, 0)],
+        (4, 5): [run(y_final, 1)],
         (6, 0): [run(pairs, 2)],
     }
 
     def later(step, point, work):
-        plan.setdefault((step, point), []).append(work)
-
+        if step < STEPS:
+            plan.setdefault((step, point), []).append(work)
+
+    for b in range(STEPS):
+        if b % 2 == 0:
+            stages = (
+                (2, 1, y_second), (2, 1, x_second), (2, 4, y_third), (2, 4, x_third),
+                (3, 6, y_mid), (3, 6, x_mid), (4, 2, y_final), (4, 2, x_final),
+            )
+        else:
+            stages = (
+                (1, 2, y_second), (1, 3, x_second), (1, 6, y_third), (2, 4, x_third),
+                (3, 1, y_mid), (3, 2, x_mid), (3, 3, y_final), (3, 4, x_final),
+            )
+        if b == STEPS - 3:
+            stages = tuple(((2, 6, x_third) if work is x_third else (lag, point, work)) for lag, point, work in stages)
+        for lag, point, work in stages:
+            if b > 1:
+                later(b + lag, point, run(work, b))
+    later(STEPS - 1, 6, run(y_second, STEPS - 2))
     for b in range(STEPS):
         later(b, 4, run(y_first, b))
         if b > 1:
             later(b, 5, run(x_first, b, 0))
-            later(b + 1, 1, run(x_first, b, 1))
-    for step in range(STEPS):
-        for lag, point, work in (
-            (3, 1, x_mid), (3, 1, y_mid), (2, 3, y_third), (2, 3, x_third),
-            (1, 3, y_second), (1, 4, x_second), (3, 6, y_final), (3, 6, x_final),
-        ):
-            if step - lag > 1:
-                later(step, point, run(work, step - lag))
-    for b in range(2):
-        later(b + 1, 4, run(y_second, b))
-        later(b + 3, 1, run(y_third, b))
-        later(b + 4, 1, run(y_mid, b))
-        later(b + 5, 1, run(y_final, b))
+            if b % 2 == 0:
+                later(b + 1, 3, run(x_first, b, 1))
+            else:
+                plan.setdefault((b + 1, 1), []).insert(0, run(x_first, b, 1))
 
     def batch(b, carry):
         def hook(point):
@@ -567,32 +608,37 @@
         zz = (z + batch_z(b // 2)) % RING
         rows = pl.ds(pl.multiple_of((b % 2) * HALF, HALF), HALF)
         hook(0)
+
         for i in range(HID // TILE):
-            hidden(zz, rows, i)
-            if i == 0:
-
-                @pl.when(b > 0)
-                def _():
-                    join(b + 3, (b + 1) % 2, 3)
-
-            hook(1 + i)
-        backs(b, hook)
+
+            @pl.when(b == 0)
+            def _():
+                hidden_owners((3, 1, 2), i)
+
+            @pl.when((b % 2 == 0) & (b > 0))
+            def _():
+                hidden_row(zz, i)
+                if i == 0:
+                    join(b + 3, 1, 3)
+
+            if i < 2:
+                hook(1 + i)
+        backs(b, rows, hook)
         return carry
 
     lax.fori_loop(0, STEPS, batch, 0)
     join(STEPS - 1, (STEPS - 1) % 2, 3)
     final = STEPS - 1
     x_first(final, 1)
-    x_mid(final - 2)
-    y_mid(final - 2)
+    x_second(final - 1)
     y_second(final)
+    y_final(final - 3)
+    x_final(final - 3)
     x_second(final)
     y_third(final - 1)
     x_third(final - 1)
     y_final(final - 2)
     x_final(final - 2)
-    y_mid(final - 1)
-    x_mid(final - 1)
     y_third(final)
     x_third(final)
     for b in (final - 1, final):
@@ -613,7 +659,7 @@
         blocks = (sum(sent.values()) - small) // block
         assert blocks * block + small == sum(sent.values())
         assert blocks == 60 and small == 15 * INFO * OWN
-        for group, ref in enumerate((xall.at[:, :, pl.ds(0, 15)], facts.at[pl.ds(0, 15)])):
+        for group, ref in enumerate((xall.at[:, pl.ds(0, 15)], facts.at[pl.ds(0, 15)])):
             pltpu.make_async_remote_copy(
                 src_ref=ref, dst_ref=ref, send_sem=gsem.at[group], recv_sem=rsem.at[0],
                 device_id=device(0, 0, 0, other), device_id_type=MESH,
@@ -626,14 +672,14 @@
     count = len(IDS)
     scratch = [
         (HID, WIDTH), (HID, WIDTH), (HID, WIDTH),
-        (BATCH, HID), (RING * RING, OWN, HID),
+        (RING, OWN, HID), (RING * RING, OWN, HID),
         (4, 4, BATCH, CHUNK), (4, 2, BATCH, CHUNK), (2, 4, BATCH, CHUNK),
         (2, 2, 128, CHUNK), (6, 2, 128, LANES),
         (2, 2, BATCH, CHUNK), (6, 2, BATCH, LANES),
         (2, BATCH, CHUNK), (6, BATCH, LANES),
-        (2, 2, 32, CHUNK), (6, 2, 32, LANES), (2, 2, HALF, CHUNK), (6, 2, HALF, LANES), (3, HALF, LANES),
+        (2, 2, 32, CHUNK), (6, 2, 32, LANES), (2, 2, HALF, CHUNK), (6, 2, HALF, LANES), (3, 3, HALF, LANES),
         (6, 2, 4, 32, LANES), (6, 2, 4, HALF, LANES),
-        (6, 4, HALF, LANES), (6, 2, 32, LANES), (6, 2, HALF, LANES), (3, HALF, LANES),
+        (6, 4, HALF, LANES), (6, 2, 32, LANES), (6, 2, HALF, LANES), (3, 3, HALF, LANES),
     ]
     return pl.pallas_call(
         kernel,
@@ -641,13 +687,13 @@
         in_specs=[pl.BlockSpec(memory_space=pl.ANY)] * 6,
         out_specs=pl.BlockSpec(memory_space=pltpu.VMEM),
         scratch_shapes=[
-            pltpu.VMEM((2, 2, 16, OWN, QUART), bf16), pltpu.VMEM((16, INFO, OWN), bf16),
+            pltpu.VMEM((2, 16, OWN, 2 * QUART), bf16), pltpu.VMEM((16, INFO, OWN), bf16),
             pltpu.VMEM((TOP, OWN), f32), pltpu.VMEM((TOP, OWN), jnp.int32),
         ]
         + [pltpu.VMEM(shape, bf16) for shape in scratch]
         + [pltpu.VMEM((OWN, CHUNK), f32)]
         + [pltpu.VMEM((6, HALF, LANES), bf16)] * 4
-        + [dma((9,)), dma((2,)), dma((count + 11,)), dma((2, 4)), dma((2, 4)), dma((74,)), dma((74,))],
+        + [dma((9,)), dma((2,)), dma((count + 11,)), dma((2, 4)), dma((2, 4)), dma((94,)), dma((94,))],
         compiler_params=pltpu.CompilerParams(
             collective_id=0, has_side_effects=True, vmem_limit_bytes=67043328
         ),

time: 114 us -> 111 us (0.974)
  Pallas kernels: 112 us -> 109 us
    pallas_call x1, Pallas kernels: 112 us -> 109 us  [local(): pl.pallas_call(kernel, out_shape=jax.ShapeDtypeStruct((OWN, CHUNK), bf16)...]
where the time goes in v4:
time: 111 us; the launch traced here: 110 us
  Pallas kernels  109 us (98%)
  local copies, waits for them, and re-layouts  1.57 us (1%)
    pallas_call x1, Pallas kernels, local(): pl.pallas_call(kernel, out_shape=jax.ShapeDtypeStruct((OWN, CHUNK), bf16)...  109 us

profile of v4, /device:TPU:0, one launch (start us, length us, event | category | flops | bytes accessed | tf_op | source)
XLA Modules:
  0.0 110.5 jit_solution(9823665384550019478)
XLA Ops:
  0.0 108.9 %shard_map.64 = bf16[128,512]{1,0:T(8,128)(2,1)} custom-call(bf16[128,4096]{1,0:T(8,128)(2,1)} %tokens.1, f32[8,128]{1,0:T(8,128)} %bitcast.8, s32[8,128]{1,0:T(8,128)} %bitcast.9, bf16[768,4096]{1,0:T(8,128)(2,1)} %bitcast.5, bf16[768,4096]{1,0:T(8,128)(2,1)} %bitcast.6, bf16[768,4096]{1,0:T(8,128)(2,1)} %bitcast.7), custom_call_target="tpu_custom_call" | custom-call | tf_op jit(solution)/shard_map/pallas_call | solution.py:684
  108.9 1.6 %copy.8 = bf16[128,512]{1,0:T(8,128)(2,1)} copy(bf16[128,512]{1,0:T(8,128)(2,1)} %shard_map.64) | data formatting | bytes 262144

commit v5 on v4

--- a/solution.py
+++ b/solution.py
@@ -202,12 +202,12 @@
         ]
 
     def direct(b):
-        return b >= STEPS - 3
+        return b >= STEPS - 4
 
     def y_last(b, stage):
         if direct(b):
             return [
-                queued(("ydirect", b, d), tot(b).at[owner_rows(d, 0, HALF)], xs3.at[b - STEPS + 3, d - 1], device(0, d, 0, c))
+                queued(("ydirect", b, d), tot(b).at[owner_rows(d, 0, HALF)], xs3.at[b - STEPS + 4, d - 1], device(0, d, 0, c))
                 for d in (2, 1, 3)
             ]
         if stage == 0:
@@ -228,9 +228,7 @@
         lanes = pl.ds(0, wide(b))
         for n in range(2):
             rows = pl.ds(n * 128, 128)
-            mine[b % 4, 1 + n, rows, lanes] = (
-                mine[b % 4, 1 + n, rows, lanes].astype(f32) + y1(b)[n].astype(f32)
-            ).astype(bf16)
+            mine[b % 4, 1 + n, rows, lanes] = mine[b % 4, 1 + n, rows, lanes] + y1(b)[n]
         begin(y_copies(b, 1))
 
     @scoped("y_third")
@@ -257,7 +255,7 @@
     def y_final(b):
         finish(y_last(b, 1))
         value = tot(b)[owner_rows(0, 0, HALF)].astype(f32)
-        for ref in [xs3.at[b - STEPS + 3, n] for n in range(3)] if direct(b) else [xs2(b).at[n] for n in range(2)]:
+        for ref in [xs3.at[b - STEPS + 4, n] for n in range(3)] if direct(b) else [xs2(b).at[n] for n in range(2)]:
             value = value + ref[...].astype(f32)
         if b < 2:
             kept[pl.ds(b * HALF, HALF)] = value
@@ -286,7 +284,7 @@
     def x_last(b, stage):
         if direct(b):
             return [
-                queued(("xdirect", b, i), wrow.at[b - 2, i], ys3.at[b - STEPS + 3, i], device(0, 0, ORDER[i], c)) for i in range(3)
+                queued(("xdirect", b, i), wrow.at[b - 2, i], ys3.at[b - STEPS + 4, i], device(0, 0, ORDER[i], c)) for i in range(3)
             ]
         if stage == 0:
             pieces = [(wrow.at[b - 2, 0, pl.ds(32 * n, 32)], ys1.at[b - 2, n]) for n in range(2)]
@@ -307,9 +305,7 @@
             for n in range(2):
                 rows = owner_rows((1, 3)[n], 32 * n, 32)
                 for i in (2 * p, 2 * p + 1):
-                    mine[b % 4, i, rows, upper] = (
-                        mine[b % 4, i, rows, upper].astype(f32) + xg1[b - 2, n, i].astype(f32)
-                    ).astype(bf16)
+                    mine[b % 4, i, rows, upper] = mine[b % 4, i, rows, upper] + xg1[b - 2, n, i]
             begin(x_copies(b, 1, p))
 
     @scoped("x_third")
@@ -340,7 +336,7 @@
     def x_final(b):
         finish(x_last(b, 1))
         value = wrow[b - 2, 3].astype(f32)
-        for ref in [ys3.at[b - STEPS + 3, n] for n in range(3)] if direct(b) else [ys2.at[b - 2, n] for n in range(2)]:
+        for ref in [ys3.at[b - STEPS + 4, n] for n in range(3)] if direct(b) else [ys2.at[b - 2, n] for n in range(2)]:
             value = value + ref[...].astype(f32)
         leave_x[b - 2] = value.astype(bf16)
         z_copy(b, 1).start()
@@ -415,7 +411,7 @@
     def join(b, s, i):
         with jax.named_scope("join"):
             d_copy(s, i).wait()
-        mine[b % 4, i] = (chunk[i, c].astype(f32) + dgot[s, i].astype(f32)).astype(bf16)
+        mine[b % 4, i] = chunk[i, c] + dgot[s, i]
 
     def backs(b, rows, hook):
         s = b % 2
@@ -557,9 +553,9 @@
         (2, 6): [bb(2, 3), bb(2, 1)],
         (3, 6): [run(y_mid, 0), run(y_third, 1)],
         (4, 0): [run(pairs, 3)],
-        (4, 3): [a(2, 0), a(2, 3), a(2, 1), bb(2, 2), a(2, 2)],
-        (4, 2): [run(y_mid, 1), run(y_final, 0)],
-        (4, 5): [run(y_final, 1)],
+        (4, 3): [a(2, 0), a(2, 3), a(2, 1), bb(2, 2), a(2, 2), run(y_mid, 1)],
+        (5, 3): [run(y_final, 0)],
+        (5, 6): [run(y_final, 1)],
         (6, 0): [run(pairs, 2)],
     }
 
@@ -580,6 +576,10 @@
             )
         if b == STEPS - 3:
             stages = tuple(((2, 6, x_third) if work is x_third else (lag, point, work)) for lag, point, work in stages)
+        if b == 2:
+            stages = tuple(((2, 2, x_second) if work is x_second else (lag, point, work)) for lag, point, work in stages)
+        if b >= STEPS - 4:
+            stages = tuple(item for item in stages if item[2] not in (y_mid, x_mid))
         for lag, point, work in stages:
             if b > 1:
                 later(b + lag, point, run(work, b))
@@ -677,9 +677,9 @@
         (2, 2, 128, CHUNK), (6, 2, 128, LANES),
         (2, 2, BATCH, CHUNK), (6, 2, BATCH, LANES),
         (2, BATCH, CHUNK), (6, BATCH, LANES),
-        (2, 2, 32, CHUNK), (6, 2, 32, LANES), (2, 2, HALF, CHUNK), (6, 2, HALF, LANES), (3, 3, HALF, LANES),
+        (2, 2, 32, CHUNK), (6, 2, 32, LANES), (2, 2, HALF, CHUNK), (6, 2, HALF, LANES), (4, 3, HALF, LANES),
         (6, 2, 4, 32, LANES), (6, 2, 4, HALF, LANES),
-        (6, 4, HALF, LANES), (6, 2, 32, LANES), (6, 2, HALF, LANES), (3, 3, HALF, LANES),
+        (6, 4, HALF, LANES), (6, 2, 32, LANES), (6, 2, HALF, LANES), (4, 3, HALF, LANES),
     ]
     return pl.pallas_call(
         kernel,
@@ -693,7 +693,7 @@
         + [pltpu.VMEM(shape, bf16) for shape in scratch]
         + [pltpu.VMEM((OWN, CHUNK), f32)]
         + [pltpu.VMEM((6, HALF, LANES), bf16)] * 4
-        + [dma((9,)), dma((2,)), dma((count + 11,)), dma((2, 4)), dma((2, 4)), dma((94,)), dma((94,))],
+        + [dma((9,)), dma((2,)), dma((count + 11,)), dma((2, 4)), dma((2, 4)), dma((100,)), dma((100,))],
         compiler_params=pltpu.CompilerParams(
             collective_id=0, has_side_effects=True, vmem_limit_bytes=67043328
         ),

time: 111 us -> 108 us (0.973)
  Pallas kernels: 109 us -> 107 us
    pallas_call x1, Pallas kernels: 109 us -> 107 us  [local(): pl.pallas_call(kernel, out_shape=jax.ShapeDtypeStruct((OWN, CHUNK), bf16)...]
where the time goes in v5:
time: 108 us
  Pallas kernels  107 us (99%)
  local copies, waits for them, and re-layouts  1.57 us (1%)
    pallas_call x1, Pallas kernels, local(): pl.pallas_call(kernel, out_shape=jax.ShapeDtypeStruct((OWN, CHUNK), bf16)...  107 us

profile of v5, /device:TPU:0, one launch (start us, length us, event | category | flops | bytes accessed | tf_op | source)
XLA Modules:
  0.0 108.3 jit_solution(14574927375602646237)
XLA Ops:
  0.0 106.7 %shard_map.64 = bf16[128,512]{1,0:T(8,128)(2,1)} custom-call(bf16[128,4096]{1,0:T(8,128)(2,1)} %tokens.1, f32[8,128]{1,0:T(8,128)} %bitcast.8, s32[8,128]{1,0:T(8,128)} %bitcast.9, bf16[768,4096]{1,0:T(8,128)(2,1)} %bitcast.5, bf16[768,4096]{1,0:T(8,128)(2,1)} %bitcast.6, bf16[768,4096]{1,0:T(8,128)(2,1)} %bitcast.7), custom_call_target="tpu_custom_call" | custom-call | tf_op jit(solution)/shard_map/pallas_call | solution.py:684
  106.7 1.6 %copy.8 = bf16[128,512]{1,0:T(8,128)(2,1)} copy(bf16[128,512]{1,0:T(8,128)(2,1)} %shard_map.64) | data formatting | bytes 262144

commit v6 on v5

--- a/solution.py
+++ b/solution.py
@@ -277,7 +277,7 @@
                 for n in range(2)
             ]
         return [
-            queued(("x", b % 2 + b // (STEPS - 1), stage, n, p), src, dst, device(0, (1, 3)[n], 0, c))
+            queued(("x", b % 4, stage, n, p), src, dst, device(0, (1, 3)[n], 0, c))
             for n, (src, dst) in enumerate(pieces)
         ]
 
@@ -574,7 +574,7 @@
                 (1, 2, y_second), (1, 3, x_second), (1, 6, y_third), (2, 4, x_third),
                 (3, 1, y_mid), (3, 2, x_mid), (3, 3, y_final), (3, 4, x_final),
             )
-        if b == STEPS - 3:
+        if b % 2:
             stages = tuple(((2, 6, x_third) if work is x_third else (lag, point, work)) for lag, point, work in stages)
         if b == 2:
             stages = tuple(((2, 2, x_second) if work is x_second else (lag, point, work)) for lag, point, work in stages)
@@ -693,7 +693,7 @@
         + [pltpu.VMEM(shape, bf16) for shape in scratch]
         + [pltpu.VMEM((OWN, CHUNK), f32)]
         + [pltpu.VMEM((6, HALF, LANES), bf16)] * 4
-        + [dma((9,)), dma((2,)), dma((count + 11,)), dma((2, 4)), dma((2, 4)), dma((100,)), dma((100,))],
+        + [dma((9,)), dma((2,)), dma((count + 11,)), dma((2, 4)), dma((2, 4)), dma((108,)), dma((108,))],
         compiler_params=pltpu.CompilerParams(
             collective_id=0, has_side_effects=True, vmem_limit_bytes=67043328
         ),

time: 108 us -> 109 us (level)
  no operation moved by 1% of the time
where the time goes in v6:
time: 109 us; the launch traced here: 108 us
  Pallas kernels  107 us (98%)
  local copies, waits for them, and re-layouts  1.57 us (1%)
    pallas_call x1, Pallas kernels, local(): pl.pallas_call(kernel, out_shape=jax.ShapeDtypeStruct((OWN, CHUNK), bf16)...  107 us

profile of v6, /device:TPU:0, one launch (start us, length us, event | category | flops | bytes accessed | tf_op | source)
XLA Modules:
  0.0 108.4 jit_solution(13799127657094290446)
XLA Ops:
  0.0 106.8 %shard_map.64 = bf16[128,512]{1,0:T(8,128)(2,1)} custom-call(bf16[128,4096]{1,0:T(8,128)(2,1)} %tokens.1, f32[8,128]{1,0:T(8,128)} %bitcast.8, s32[8,128]{1,0:T(8,128)} %bitcast.9, bf16[768,4096]{1,0:T(8,128)(2,1)} %bitcast.5, bf16[768,4096]{1,0:T(8,128)(2,1)} %bitcast.6, bf16[768,4096]{1,0:T(8,128)(2,1)} %bitcast.7), custom_call_target="tpu_custom_call" | custom-call | tf_op jit(solution)/shard_map/pallas_call | solution.py:684
  106.8 1.6 %copy.8 = bf16[128,512]{1,0:T(8,128)(2,1)} copy(bf16[128,512]{1,0:T(8,128)(2,1)} %shard_map.64) | data formatting | bytes 262144
